TPU v7x, 256 devices: a 8x8x2 block of a 8x8x16 slice. The times are simulated.
256 devices in a mesh: groups: 2 (over z), gx: 128 (over x, y, core).
Axes of the slice: x: 8, y: 8, z: 2, core: 2. Of those that a mesh axis runs over, the one named last changes fastest.
The devices are a block of a 8x8x16 slice.
Arguments:
- fields: float32 [3, 1024, 32768], P(None, 'groups', 'gx'), parts along dimension 1, may hold values from -0.7 to 1.4, as said below
- friction: float32 [1024, 32768], P('groups', 'gx'), parts along dimension 0, may hold values from 0.2 to 1.6
- wet_mask: int32 [1024, 32768], P('groups', 'gx'), parts along dimension 0, may hold values from 0 to 1, as said below
- owner_table: int32 [4, 128], P('groups'), parts along dimension 0, may hold values from 0 to 127, as said below
Outputs:
- final_fields: float32 [3, 1024, 32768], P(None, 'groups', 'gx'), parts along dimension 1
- owned_depth: float32 [1024, 32768], P('groups', 'gx'), parts along dimension 0
There are 2 independent parts, one for each index of `groups`. A program takes and returns all parts, laid end to end along the dimension named above; each array names one. Nothing has to cross between parts.
Inputs may be any that keep to these rules, and one draw needn't show every extreme that they name: fields[0] is the depth, 0.6 to 1.4; fields[1] and fields[2] are the momenta, -0.7 to 0.7. `wet_mask`: land covers whole tiles: in each home column the tiles that hold water are the first ones (tile rows 0 up to some row, at least row 0), and some tiles hold no water. In each tile row and each aligned block of 8 home columns, owner_table[r, c] = c XOR k for one k from 0 to 7, so every device owns exactly one tile of each tile row.
All inputs are finite; a program needn't handle non-finite values.
Results may differ from a plain program's by a relative error of at most 0.0003.
Values sent between devices are 32-bit elements; how exact they have to be, the bound alone decides.
A program may use at most 64 MiB of HBM per device.

v0:
```python
import functools

import jax
import jax.numpy as jnp
from jax import lax
from jax.experimental import pallas as pl
from jax.experimental.pallas import tpu as pltpu
from jax.sharding import PartitionSpec as P

STEPS = 2
PAD = 8
CHUNKS = 4
LANES = 128

gravity_half = 0.5
depth_floor = 0.25
flux_factor = 0.1
time_step = 0.25


def advance(state, wet, damping, east, west, south, north):
    h, p, q = state
    inverse = 1.0 / jnp.maximum(h, depth_floor)
    u = p * inverse
    v = q * inverse
    pressure = gravity_half * h * h
    cross = q * u
    flux_p = p * u + pressure
    flux_q = q * v + pressure

    def gather(cell, flux_east, flux_south):
        quarter = 0.25 * cell
        along = flux_factor * flux_east
        down = flux_factor * flux_south
        return (east(quarter - along) + west(quarter + along)) + (
            south(quarter - down) + north(quarter + down)
        )

    return (
        wet * gather(h, p, q),
        damping * gather(p, flux_p, cross),
        damping * gather(q, cross, flux_q),
    )


def masks(openness):
    wet = jnp.where(openness > 0.0, 1.0, 0.0)
    return wet, wet / (1.0 + time_step * openness)


def flip(me, bit):
    stride = 2 ** bit
    return me + stride - 2 * stride * ((me // stride) % 2)


def kernel(
    axis,
    count,
    fields_ref,
    friction_ref,
    wet_ref,
    owner_ref,
    out_fields,
    out_depth,
    state,
    fric,
    mask,
    first,
    got_one,
    mid,
    got_mid,
    second,
    got_two,
    packed,
    halo_left,
    halo_right,
    edge,
    edge_turn,
    edge_first,
    edge_mid,
    edge_second,
    edge_got,
    edge_final,
    edge_wide,
    load_sem,
    send_sem,
    recv_sem,
    halo_send,
    halo_recv,
    edge_send,
    edge_recv,
):
    rows, cols = friction_ref.shape
    tile = cols
    tile_rows = rows // tile
    chunk = tile // CHUNKS
    me = lax.axis_index(axis)
    left = lax.rem(me + count - 1, count)
    right = lax.rem(me + 1, count)
    partner = [flip(me, bit) for bit in range(3)]

    loads = [
        pltpu.make_async_copy(
            fields_ref.at[plane], state.at[plane, pl.ds(PAD, rows), :], load_sem.at[plane]
        )
        for plane in range(3)
    ]
    loads.append(pltpu.make_async_copy(friction_ref, fric.at[pl.ds(PAD, rows), :], load_sem.at[3]))
    loads.append(pltpu.make_async_copy(wet_ref, mask.at[pl.ds(PAD, rows), :], load_sem.at[4]))
    for load in loads:
        load.start()

    barrier = pltpu.get_barrier_semaphore()
    peers = [left, right] + partner
    for peer in peers:
        pl.semaphore_signal(
            barrier, inc=1, device_id={axis: peer}, device_id_type=pl.DeviceIdType.MESH
        )

    zero_rows = jnp.zeros((PAD, cols), jnp.float32)
    for start in (0, PAD + rows):
        for plane in range(3):
            state[plane, start : start + PAD, :] = zero_rows
        fric[start : start + PAD, :] = zero_rows
        mask[start : start + PAD, :] = jnp.zeros((PAD, cols), jnp.int32)
    edge[...] = jnp.zeros_like(edge)
    edge_wide[...] = jnp.zeros_like(edge_wide)

    def bit_of(tile_row, bit):
        own = owner_ref[tile_row, me]
        return ((own // 2 ** bit) + (me // 2 ** bit)) % 2

    early = [2 if tile_row % 2 == 0 else 1 for tile_row in range(tile_rows)]
    late = [3 - bit for bit in early]

    def remote(src, dst, sems, bit):
        return pltpu.make_async_remote_copy(
            src_ref=src,
            dst_ref=dst,
            send_sem=sems[0],
            recv_sem=sems[1],
            device_id={axis: partner[bit]},
            device_id_type=pl.DeviceIdType.MESH,
        )

    def exchange(stage, tile_row, i):
        src, dst = ((first, got_one), (mid, got_mid), (second, got_two))[stage]
        bit = (early[tile_row], 0, late[tile_row])[stage]
        where = pl.ds(pl.multiple_of(i * chunk, chunk), chunk)
        return remote(
            src.at[tile_row, where, :],
            dst.at[tile_row, where, :],
            (send_sem.at[stage, tile_row, i], recv_sem.at[stage, tile_row, i]),
            bit,
        )

    def shift(axis_number, amount, size):
        return lambda a: pltpu.roll(a, amount % size, axis_number)

    def compute(tile_row, i):
        span = chunk + 2 * PAD
        at = pl.multiple_of(tile_row * tile + i * chunk, PAD)
        where = pl.ds(at, span)
        openness = mask[where, :].astype(jnp.float32) * fric[where, :]
        wet, damping = masks(openness)
        values = tuple(state[plane, where, :] * wet for plane in range(3))
        for _ in range(STEPS):
            values = advance(
                values,
                wet,
                damping,
                shift(1, -1, cols),
                shift(1, 1, cols),
                shift(0, -1, span),
                shift(0, 1, span),
            )
        here = pl.ds(at, chunk)
        for plane in range(3):
            out_fields[plane, here, :] = values[plane][PAD : PAD + chunk]
        first[tile_row, pl.ds(pl.multiple_of(i * chunk, chunk), chunk), :] = values[0][
            PAD : PAD + chunk
        ]

    for load in loads:
        load.wait()

    for tile_row in range(tile_rows):
        compute(tile_row, 0)
    pl.semaphore_wait(barrier, len(peers))
    for tile_row in range(tile_rows):
        exchange(0, tile_row, 0).start()

    lane = lax.broadcasted_iota(jnp.int32, (LANES, LANES), 1)

    @pl.loop(0, rows // LANES)
    def _(block):
        where = pl.ds(pl.multiple_of(PAD + block * LANES, PAD), LANES)
        open_sides = []
        for low in (0, cols - LANES):
            cut = pl.ds(low, LANES)
            open_sides.append(mask[where, cut].astype(jnp.float32) * fric[where, cut])
        result = jnp.zeros((LANES, LANES), jnp.float32)
        for side, low in enumerate((0, cols - LANES)):
            wet, _ = masks(open_sides[side])
            cut = pl.ds(low, LANES)
            planes = [state[plane, where, cut] * wet for plane in range(3)] + [open_sides[side]]
            for number, values in enumerate(planes):
                for inner in range(2):
                    if side == 0:
                        source = 2 * inner
                    else:
                        source = LANES - 2 - 2 * inner
                    target = 16 * inner + 8 * side + 2 * number
                    moved = pltpu.roll(values, (target - source) % LANES, 1)
                    result = jnp.where((lane >= target) & (lane < target + 2), moved, result)
        packed[:, pl.ds(pl.multiple_of(block * LANES, LANES), LANES)] = result.T[0:32]

    halo_copies = [
        pltpu.make_async_remote_copy(
            src_ref=packed.at[pl.ds(8 * side, 8), :],
            dst_ref=(halo_right, halo_left)[side],
            send_sem=halo_send.at[side],
            recv_sem=halo_recv.at[side],
            device_id={axis: (left, right)[side]},
            device_id_type=pl.DeviceIdType.MESH,
        )
        for side in range(2)
    ]
    for copy in halo_copies:
        copy.start()

    @pl.loop(1, CHUNKS)
    def _(i):
        for tile_row in range(tile_rows):
            compute(tile_row, i)
            exchange(0, tile_row, i).start()

    for copy in halo_copies:
        copy.wait_recv()

    keep_left = jnp.where(me > 0, 1.0, 0.0)
    keep_right = jnp.where(me < count - 1, 1.0, 0.0)
    for number in range(4):
        pair = pl.ds(2 * number, 2)
        edge[number, 0:2, :] = halo_left[pair, :] * keep_left
        edge[number, 2:4, :] = packed[pl.ds(2 * number, 2), :]
        edge[number, 4:6, :] = packed[pl.ds(16 + 2 * number, 2), :]
        edge[number, 8:10, :] = packed[pl.ds(24 + 2 * number, 2), :]
        edge[number, 10:12, :] = packed[pl.ds(8 + 2 * number, 2), :]
        edge[number, 12:14, :] = halo_right[pair, :] * keep_right

    place = lax.broadcasted_iota(jnp.int32, (16, rows), 1)
    wet, damping = masks(edge[3])
    values = tuple(edge[plane] for plane in range(3))
    for _ in range(STEPS):
        values = advance(
            values,
            wet,
            damping,
            shift(0, -1, 16),
            shift(0, 1, 16),
            lambda a: jnp.where(place == rows - 1, 0.0, pltpu.roll(a, rows - 1, 1)),
            lambda a: jnp.where(place == 0, 0.0, pltpu.roll(a, 1, 1)),
        )
    edge_turn[...] = jnp.zeros_like(edge_turn)
    for plane in range(3):
        edge_turn[16 * plane : 16 * plane + 16, :] = values[plane]
    for tile_row in range(tile_rows):
        cut = pl.ds(tile_row * tile, tile)
        edge_first[4 * tile_row : 4 * tile_row + 2, :] = edge_turn[2:4, cut]
        edge_first[4 * tile_row + 2 : 4 * tile_row + 4, :] = edge_turn[10:12, cut]

    edge_bits = (2, 0, 1)
    edge_sends = (edge_first, edge_mid, edge_second)

    def edge_exchange(stage):
        return remote(
            edge_sends[stage],
            edge_got.at[stage],
            (edge_send.at[stage], edge_recv.at[stage]),
            edge_bits[stage],
        )

    edge_line = lax.broadcasted_iota(jnp.int32, (8, tile), 0)

    def edge_select(stage):
        bit = edge_bits[stage]
        taken = jnp.where(edge_line < 4, bit_of(0, bit), bit_of(1, bit))
        return jnp.where(taken == 1, edge_got[stage], edge_sends[stage][...])

    edge_exchange(0).start()

    narrow = lax.broadcasted_iota(jnp.int32, (LANES, LANES), 1)

    @pl.loop(0, rows // LANES)
    def _(block):
        where = pl.ds(pl.multiple_of(block * LANES, LANES), LANES)
        turned = edge_turn[:, where].T
        for plane in range(3):
            on_left = pltpu.roll(turned, (-16 * plane - 2) % LANES, 1)
            cut = pl.ds(0, LANES)
            out_fields[plane, where, cut] = jnp.where(
                narrow < 2, on_left, out_fields[plane, where, cut]
            )
            on_right = pltpu.roll(turned, (LANES - 2 - 16 * plane - 10) % LANES, 1)
            cut = pl.ds(cols - LANES, LANES)
            out_fields[plane, where, cut] = jnp.where(
                narrow >= LANES - 2, on_right, out_fields[plane, where, cut]
            )

    def pick(stage, tile_row, i):
        src, dst = ((first, got_one), (mid, got_mid), (second, got_two))[stage]
        bit = (early[tile_row], 0, late[tile_row])[stage]
        where = pl.ds(i * chunk, chunk)
        taken = jnp.full((chunk, tile), bit_of(tile_row, bit), jnp.int32)
        return jnp.where(taken == 1, dst[tile_row, where, :], src[tile_row, where, :])

    for i in range(CHUNKS + 1):
        if i < CHUNKS:
            for tile_row in range(tile_rows):
                exchange(0, tile_row, i).wait_recv()
                mid[tile_row, i * chunk : (i + 1) * chunk, :] = pick(0, tile_row, i)
                exchange(1, tile_row, i).start()
        if i == CHUNKS - 1:
            edge_exchange(0).wait_recv()
            edge_mid[...] = edge_select(0)
            edge_exchange(1).start()
        if i == CHUNKS:
            edge_exchange(1).wait_recv()
            edge_second[...] = edge_select(1)
            edge_exchange(2).start()
        if i >= 1:
            for tile_row in range(tile_rows):
                exchange(1, tile_row, i - 1).wait_recv()
                second[tile_row, (i - 1) * chunk : i * chunk, :] = pick(1, tile_row, i - 1)
                exchange(2, tile_row, i - 1).start()

    edge_exchange(2).wait_recv()
    edge_final[...] = jnp.zeros_like(edge_final)
    edge_final[0:8, :] = edge_select(2)
    for tile_row in range(tile_rows):
        for block in range(tile // LANES):
            turned = edge_final[:, block * LANES : (block + 1) * LANES].T
            where = pl.ds(block * LANES, LANES)
            edge_wide[tile_row, where, 0:LANES] = pltpu.roll(turned, (-4 * tile_row) % LANES, 1)
            edge_wide[tile_row, where, cols - LANES : cols] = pltpu.roll(
                turned, (LANES - 2 - 4 * tile_row - 2) % LANES, 1
            )

    column = lax.broadcasted_iota(jnp.int32, (chunk, cols), 1)
    inside = (column >= 2) & (column < cols - 2)
    for i in range(CHUNKS):
        for tile_row in range(tile_rows):
            exchange(2, tile_row, i).wait_recv()
            out_depth[tile_row * tile + i * chunk : tile_row * tile + (i + 1) * chunk, :] = jnp.where(
                inside, pick(2, tile_row, i), edge_wide[tile_row, i * chunk : (i + 1) * chunk, :]
            )

    for copy in halo_copies:
        copy.wait_send()
    for stage in range(3):
        edge_exchange(stage).wait_send()
        for tile_row in range(tile_rows):
            for i in range(CHUNKS):
                exchange(stage, tile_row, i).wait_send()


def solution(mesh):
    axis = "gx"
    count = mesh.shape[axis]

    def body(fields, friction, wet_mask, owner_table):
        rows, cols = friction.shape
        tile_rows = rows // cols
        tiles = (tile_rows, cols, cols)
        padded = rows + 2 * PAD
        f32 = jnp.float32
        scratch = [
            pltpu.VMEM((3, padded, cols), f32),
            pltpu.VMEM((padded, cols), f32),
            pltpu.VMEM((padded, cols), jnp.int32),
            pltpu.VMEM(tiles, f32),
            pltpu.VMEM(tiles, f32),
            pltpu.VMEM(tiles, f32),
            pltpu.VMEM(tiles, f32),
            pltpu.VMEM(tiles, f32),
            pltpu.VMEM(tiles, f32),
            pltpu.VMEM((32, rows), f32),
            pltpu.VMEM((8, rows), f32),
            pltpu.VMEM((8, rows), f32),
            pltpu.VMEM((4, 16, rows), f32),
            pltpu.VMEM((LANES, rows), f32),
            pltpu.VMEM((8, cols), f32),
            pltpu.VMEM((8, cols), f32),
            pltpu.VMEM((8, cols), f32),
            pltpu.VMEM((3, 8, cols), f32),
            pltpu.VMEM((LANES, cols), f32),
            pltpu.VMEM(tiles, f32),
            pltpu.SemaphoreType.DMA((5,)),
            pltpu.SemaphoreType.DMA((3, tile_rows, CHUNKS)),
            pltpu.SemaphoreType.DMA((3, tile_rows, CHUNKS)),
            pltpu.SemaphoreType.DMA((2,)),
            pltpu.SemaphoreType.DMA((2,)),
            pltpu.SemaphoreType.DMA((3,)),
            pltpu.SemaphoreType.DMA((3,)),
        ]
        return pl.pallas_call(
            functools.partial(kernel, axis, count),
            out_shape=(
                jax.ShapeDtypeStruct(fields.shape, f32),
                jax.ShapeDtypeStruct(friction.shape, f32),
            ),
            in_specs=[
                pl.BlockSpec(memory_space=pl.ANY),
                pl.BlockSpec(memory_space=pl.ANY),
                pl.BlockSpec(memory_space=pl.ANY),
                pl.BlockSpec(memory_space=pltpu.SMEM),
            ],
            out_specs=(
                pl.BlockSpec(memory_space=pltpu.VMEM),
                pl.BlockSpec(memory_space=pltpu.VMEM),
            ),
            scratch_shapes=scratch,
            compiler_params=pltpu.CompilerParams(collective_id=0, has_side_effects=True),
            name="shallow_water",
        )(fields, friction, wet_mask, owner_table)

    in_specs = (P(None, "groups", axis), P("groups", axis), P("groups", axis), P("groups", None))
    out_specs = (P(None, "groups", axis), P("groups", axis))
    return jax.shard_map(body, mesh=mesh, in_specs=in_specs, out_specs=out_specs, check_vma=False)
```

profile of v0, /device:TPU:513, one launch (start us, length us, event | category | flops | bytes accessed | tf_op | source)
XLA Modules:
  0.0 49.4 jit_solution(14974750787666916047)
XLA Ops:
  0.6 45.2 %shallow_water.1 = (f32[3,512,256]{2,1,0:T(8,128)}, f32[512,256]{1,0:T(8,128)}) custom-call(f32[3,512,256]{2,1,0:T(8,128)} %fields_ref.1, f32[512,256]{1,0:T(8,128)} %friction_ref.1, s32[512,256]{1,0:T(8,128)} %wet_ref.1, s32[2,128]{1,0:T(2,128)} %owner_ref.1), custom_call_target="tpu_custom_call" | custom-call | tf_op jit(solution)/shard_map/shallow_water/pallas_call | solution.py:407
  45.9 0.0 copy-start
  45.9 2.7 %copy.8 = f32[3,512,256]{2,1,0:T(8,128)} copy(f32[3,512,256]{2,1,0:T(8,128)} %get-tuple-element.4) | data formatting | bytes 3145728
  48.6 0.0 copy-done
  48.6 0.8 %copy.9 = f32[512,256]{1,0:T(8,128)} copy(f32[512,256]{1,0:T(8,128)S(1)} %copy-done) | data formatting | bytes 1048576
Async XLA Ops:
  45.9 2.7 %copy-start = (f32[512,256]{1,0:T(8,128)S(1)}, f32[512,256]{1,0:T(8,128)}, u32[]{:S(2)}) copy-start(f32[512,256]{1,0:T(8,128)} %get-tuple-element.5) | copy-start | bytes 1572868
where the time goes:
time: 49.6 us; the launch traced here: 49.4 us
  Pallas kernels  45.2 us (91%)
  local copies, waits for them, and re-layouts  3.51 us (7%)
  between operations  0.65 us (1%)
    pallas_call x1, Pallas kernels, body(): pl.pallas_call(functools.partial(kernel, axis, count), out_shape=(jax.Sha...  45.2 us
    unnamed x4, local copies, waits for them, and re-layouts  3.51 us

commit v1 on v0

v1 whole, which is shorter than its diff:
```python
import functools

import jax
import jax.numpy as jnp
from jax import lax
from jax.experimental import pallas as pl
from jax.experimental.pallas import tpu as pltpu
from jax.sharding import PartitionSpec as P

STEPS = 2
PAD = 8
CHUNK = 64
MESSAGE = 32
LANES = 128

gravity_half = 0.5
depth_floor = 0.25
flux_factor = 0.1
time_step = 0.25


def advance(state, wet, damping, east, west, south, north):
    h, p, q = state
    inverse = 1.0 / jnp.maximum(h, depth_floor)
    u = p * inverse
    v = q * inverse
    pressure = gravity_half * h * h
    cross = q * u
    flux_p = p * u + pressure
    flux_q = q * v + pressure

    def gather(cell, flux_east, flux_south):
        quarter = 0.25 * cell
        along = flux_factor * flux_east
        down = flux_factor * flux_south
        return (east(quarter - along) + west(quarter + along)) + (
            south(quarter - down) + north(quarter + down)
        )

    return (
        wet * gather(h, p, q),
        damping * gather(p, flux_p, cross),
        damping * gather(q, cross, flux_q),
    )


def masks(openness):
    wet = jnp.where(openness > 0.0, 1.0, 0.0)
    return wet, wet / (1.0 + time_step * openness)


def kernel(
    axis,
    count,
    fields_ref,
    friction_ref,
    wet_ref,
    owner_ref,
    out_fields,
    out_depth,
    state,
    fric,
    mask,
    owner,
    first,
    inbox,
    back,
    turn,
    mine,
    other,
    packed,
    halo_left,
    halo_right,
    edge,
    edge_turn,
    edge_first,
    edge_in,
    edge_back,
    edge_give,
    edge_mine,
    edge_other,
    edge_final,
    edge_wide,
    load_sem,
    raw_send,
    relay_send,
    in_recv,
    back_send,
    back_recv,
    swap_send,
    swap_recv,
    halo_send,
    halo_recv,
):
    rows, cols = friction_ref.shape
    tile = cols
    tile_rows = rows // tile
    messages = rows // MESSAGE
    extra = messages
    MESH = pl.DeviceIdType.MESH

    me = lax.axis_index(axis)
    odd = me % 2
    position = me % 8
    chip = position // 2
    middle = ((chip + 1) // 2) % 2
    toward = me + 2 - 4 * (chip // 2)
    outward = 2 * me - toward
    sibling = me + 1 - 2 * odd
    is_middle = middle == 1
    is_end = middle == 0

    last = jnp.where(me == count - 1, 1, 0)
    lead_left = jnp.where(position == 0, 0, 1 - odd)
    follow_left = jnp.where(me == 0, 0, 1 - lead_left)
    lead_right = jnp.where(position == 7, 1, 1 - odd) * (1 - last)
    follow_right = (1 - last) * (1 - lead_right)

    loads = [
        pltpu.make_async_copy(
            fields_ref.at[plane], state.at[plane, pl.ds(PAD, rows), :], load_sem.at[plane]
        )
        for plane in range(3)
    ]
    loads.append(pltpu.make_async_copy(friction_ref, fric.at[pl.ds(PAD, rows), :], load_sem.at[3]))
    loads.append(pltpu.make_async_copy(wet_ref, mask.at[pl.ds(PAD, rows), :], load_sem.at[4]))
    loads.append(pltpu.make_async_copy(owner_ref, owner, load_sem.at[5]))
    for load in loads:
        load.start()

    barrier = pltpu.get_barrier_semaphore()

    def greet(peer):
        pl.semaphore_signal(barrier, inc=1, device_id={axis: peer}, device_id_type=MESH)

    @pl.when(is_middle)
    def _():
        greet(outward)
        greet(toward)

    @pl.when(follow_left == 1)
    def _():
        greet(me - 1)

    @pl.when(follow_right == 1)
    def _():
        greet(me + 1)

    zero_rows = jnp.zeros((PAD, cols), jnp.float32)
    for start in (0, PAD + rows):
        for plane in range(3):
            state[plane, start : start + PAD, :] = zero_rows
        fric[start : start + PAD, :] = zero_rows
        mask[start : start + PAD, :] = jnp.zeros((PAD, cols), jnp.int32)
    edge[...] = jnp.zeros_like(edge)
    edge_turn[...] = jnp.zeros_like(edge_turn)
    edge_final[...] = jnp.zeros_like(edge_final)

    def differs(tile_row, bit):
        own = owner[tile_row, me]
        return (own // 2 ** bit + me // 2 ** bit) % 2

    def remote(src, dst, send, recv, peer):
        return pltpu.make_async_remote_copy(
            src_ref=src,
            dst_ref=dst,
            send_sem=send,
            recv_sem=recv,
            device_id={axis: peer},
            device_id_type=MESH,
        )

    def span(m):
        return pl.ds(pl.multiple_of(m * MESSAGE, MESSAGE), MESSAGE)

    def raw(m, slot):
        return remote(
            first.at[span(m), :], inbox.at[slot, span(m), :], raw_send.at[m], in_recv.at[slot, m], toward
        )

    def relay(m):
        return remote(
            inbox.at[0, span(m), :], inbox.at[2, span(m), :], relay_send.at[m], in_recv.at[2, m], toward
        )

    def give(m):
        return remote(turn.at[span(m), :], back.at[span(m), :], back_send.at[m], back_recv.at[m], outward)

    def swap(m):
        return remote(mine.at[span(m), :], other.at[span(m), :], swap_send.at[m], swap_recv.at[m], sibling)

    def edge_raw(slot):
        return remote(edge_first, edge_in.at[slot], raw_send.at[extra], in_recv.at[slot, extra], toward)

    edge_relay = remote(
        edge_in.at[0], edge_in.at[2], relay_send.at[extra], in_recv.at[2, extra], toward
    )
    edge_return = remote(edge_give, edge_back, back_send.at[extra], back_recv.at[extra], outward)
    edge_swap = remote(edge_mine, edge_other, swap_send.at[extra], swap_recv.at[extra], sibling)

    halo_to_left = remote(
        packed.at[pl.ds(0, 8), :], halo_right, halo_send.at[0], halo_recv.at[0], me - 1
    )
    halo_to_right = remote(
        packed.at[pl.ds(8, 8), :], halo_left, halo_send.at[1], halo_recv.at[1], me + 1
    )

    def shift(axis_number, amount, size):
        return lambda a: pltpu.roll(a, amount % size, axis_number)

    def compute(i):
        height = CHUNK + 2 * PAD
        at = pl.multiple_of(i * CHUNK, CHUNK)
        where = pl.ds(at, height)
        openness = mask[where, :].astype(jnp.float32) * fric[where, :]
        wet, damping = masks(openness)
        values = tuple(state[plane, where, :] * wet for plane in range(3))
        for _ in range(STEPS):
            values = advance(
                values,
                wet,
                damping,
                shift(1, -1, cols),
                shift(1, 1, cols),
                shift(0, -1, height),
                shift(0, 1, height),
            )
        here = pl.ds(at, CHUNK)
        first[here, :] = values[0][PAD : PAD + CHUNK]
        for plane in range(3):
            out_fields[plane, here, :] = values[plane][PAD : PAD + CHUNK]

    for load in loads:
        load.wait()

    compute(0)
    pl.semaphore_wait(barrier, 1 + lead_left + lead_right)
    for part in range(CHUNK // MESSAGE):
        raw(part, middle).start()

    lane = lax.broadcasted_iota(jnp.int32, (LANES, LANES), 1)

    @pl.loop(0, rows // LANES)
    def _(block):
        where = pl.ds(pl.multiple_of(PAD + block * LANES, PAD), LANES)
        result = jnp.zeros((LANES, LANES), jnp.float32)
        for side, low in enumerate((0, cols - LANES)):
            cut = pl.ds(low, LANES)
            openness = mask[where, cut].astype(jnp.float32) * fric[where, cut]
            wet, _ = masks(openness)
            planes = [state[plane, where, cut] * wet for plane in range(3)] + [openness]
            for number, values in enumerate(planes):
                for inner in range(2):
                    source = LANES - 2 - 2 * inner if side else 2 * inner
                    target = 16 * inner + 8 * side + 2 * number
                    moved = pltpu.roll(values, (target - source) % LANES, 1)
                    result = jnp.where((lane >= target) & (lane < target + 2), moved, result)
        packed[:, pl.ds(pl.multiple_of(block * LANES, LANES), LANES)] = result.T[0:32]

    @pl.when(lead_left == 1)
    def _():
        halo_to_left.start()

    @pl.when(lead_right == 1)
    def _():
        halo_to_right.start()

    @pl.loop(1, rows // CHUNK)
    def _(i):
        compute(i)
        for part in range(CHUNK // MESSAGE):
            raw(i * (CHUNK // MESSAGE) + part, middle).start()

    @pl.when(follow_right == 1)
    def _():
        halo_to_left.wait_recv()
        halo_to_right.start()

    @pl.when(follow_left == 1)
    def _():
        halo_to_right.wait_recv()
        halo_to_left.start()

    @pl.when(lead_right == 1)
    def _():
        halo_to_left.wait_recv()

    @pl.when(lead_left == 1)
    def _():
        halo_to_right.wait_recv()

    for number in range(4):
        pair = pl.ds(2 * number, 2)
        edge[number, 0:2, :] = jnp.where(me > 0, halo_left[pair, :], 0.0)
        edge[number, 2:4, :] = packed[pl.ds(2 * number, 2), :]
        edge[number, 4:6, :] = packed[pl.ds(16 + 2 * number, 2), :]
        edge[number, 8:10, :] = packed[pl.ds(24 + 2 * number, 2), :]
        edge[number, 10:12, :] = packed[pl.ds(8 + 2 * number, 2), :]
        edge[number, 12:14, :] = jnp.where(me < count - 1, halo_right[pair, :], 0.0)

    place = lax.broadcasted_iota(jnp.int32, (16, rows), 1)
    wet, damping = masks(edge[3])
    values = tuple(edge[plane] for plane in range(3))
    for _ in range(STEPS):
        values = advance(
            values,
            wet,
            damping,
            shift(0, -1, 16),
            shift(0, 1, 16),
            lambda a: jnp.where(place == rows - 1, 0.0, pltpu.roll(a, rows - 1, 1)),
            lambda a: jnp.where(place == 0, 0.0, pltpu.roll(a, 1, 1)),
        )
    for plane in range(3):
        edge_turn[16 * plane : 16 * plane + 16, :] = values[plane]
    for tile_row in range(tile_rows):
        cut = pl.ds(tile_row * tile, tile)
        edge_first[4 * tile_row : 4 * tile_row + 2, :] = edge_turn[2:4, cut]
        edge_first[4 * tile_row + 2 : 4 * tile_row + 4, :] = edge_turn[10:12, cut]
    edge_raw(middle).start()

    @pl.when(is_middle)
    def _():
        @pl.loop(0, messages - 2)
        def _(m):
            raw(m, 0).wait_recv()
            relay(m).start()

        edge_raw(0).wait_recv()
        edge_relay.start()
        for m in range(messages - 2, messages):
            raw(m, 0).wait_recv()
            relay(m).start()

    @pl.loop(0, rows // LANES)
    def _(block):
        where = pl.ds(pl.multiple_of(block * LANES, LANES), LANES)
        turned = edge_turn[:, where].T
        for plane in range(3):
            on_left = pltpu.roll(turned, (-16 * plane - 2) % LANES, 1)
            cut = pl.ds(0, LANES)
            out_fields[plane, where, cut] = jnp.where(
                lane < 2, on_left, out_fields[plane, where, cut]
            )
            on_right = pltpu.roll(turned, (LANES - 2 - 16 * plane - 10) % LANES, 1)
            cut = pl.ds(cols - LANES, LANES)
            out_fields[plane, where, cut] = jnp.where(
                lane >= LANES - 2, on_right, out_fields[plane, where, cut]
            )

    moves = [differs(tile_row, 1) + 2 * differs(tile_row, 2) for tile_row in range(tile_rows)]
    flips = [differs(tile_row, 0) for tile_row in range(tile_rows)]

    def for_end(by, own, near, far):
        return jnp.where(by == 3, far, jnp.where(by == 2, near, own))

    def for_middle(by, own, end, near, far):
        return jnp.where(by == 3, near, jnp.where(by == 2, far, jnp.where(by == 1, end, own)))

    def of_row(pair, m, shape):
        value = pair[-1]
        for tile_row in reversed(range(tile_rows - 1)):
            value = jnp.where(m < (tile_row + 1) * (tile // MESSAGE), pair[tile_row], value)
        return jnp.full(shape, value, jnp.int32)

    def settle(m):
        where = span(m)
        by = of_row(moves, m, (MESSAGE, cols))

        @pl.when(is_middle)
        def _():
            raw(m, 1).wait_recv()
            relay(m).wait_recv()
            own = first[where, :]
            near = inbox[1, where, :]
            far = inbox[2, where, :]
            turn[where, :] = for_end(by, own, near, far)
            give(m).start()
            mine[where, :] = for_middle(by, own, inbox[0, where, :], near, far)

        @pl.when(is_end)
        def _():
            give(m).wait_recv()
            mine[where, :] = jnp.where(by == 0, first[where, :], back[where, :])

        swap(m).start()

    line = lax.broadcasted_iota(jnp.int32, (8, cols), 0)

    def by_line(pair):
        value = jnp.full((8, cols), pair[-1], jnp.int32)
        for tile_row in reversed(range(tile_rows - 1)):
            value = jnp.where(line < 4 * (tile_row + 1), pair[tile_row], value)
        return value

    @pl.loop(0, messages - 2)
    def _(m):
        settle(m)

    edge_by = by_line(moves)

    @pl.when(is_middle)
    def _():
        edge_raw(1).wait_recv()
        edge_relay.wait_recv()
        own = edge_first[...]
        near = edge_in[1]
        far = edge_in[2]
        edge_give[...] = for_end(edge_by, own, near, far)
        edge_return.start()
        edge_mine[...] = for_middle(edge_by, own, edge_in[0], near, far)

    @pl.when(is_end)
    def _():
        edge_return.wait_recv()
        edge_mine[...] = jnp.where(edge_by == 0, edge_first[...], edge_back[...])

    edge_swap.start()
    for m in range(messages - 2, messages):
        settle(m)

    edge_swap.wait_recv()
    edge_final[0:8, :] = jnp.where(by_line(flips) == 1, edge_other[...], edge_mine[...])
    for tile_row in range(tile_rows):
        for block in range(tile // LANES):
            turned = edge_final[:, block * LANES : (block + 1) * LANES].T
            where = pl.ds(tile_row * tile + block * LANES, LANES)
            edge_wide[where, 0:LANES] = pltpu.roll(turned, (-4 * tile_row) % LANES, 1)
            edge_wide[where, cols - LANES : cols] = pltpu.roll(
                turned, (LANES - 2 - 4 * tile_row - 2) % LANES, 1
            )

    column = lax.broadcasted_iota(jnp.int32, (MESSAGE, cols), 1)
    inside = (column >= 2) & (column < cols - 2)

    @pl.loop(0, messages)
    def _(m):
        swap(m).wait_recv()
        where = span(m)
        taken = of_row(flips, m, (MESSAGE, cols)) == 1
        value = jnp.where(taken, other[where, :], mine[where, :])
        out_depth[where, :] = jnp.where(inside, value, edge_wide[where, :])

    @pl.when((lead_left == 1) | (follow_left == 1))
    def _():
        halo_to_left.wait_send()

    @pl.when((lead_right == 1) | (follow_right == 1))
    def _():
        halo_to_right.wait_send()

    edge_raw(middle).wait_send()
    edge_swap.wait_send()

    @pl.loop(0, messages)
    def _(m):
        raw(m, middle).wait_send()
        swap(m).wait_send()

    @pl.when(is_middle)
    def _():
        edge_relay.wait_send()
        edge_return.wait_send()

        @pl.loop(0, messages)
        def _(m):
            relay(m).wait_send()
            give(m).wait_send()


def solution(mesh):
    axis = "gx"
    count = mesh.shape[axis]

    def body(fields, friction, wet_mask, owner_table):
        rows, cols = friction.shape
        padded = rows + 2 * PAD
        slots = rows // MESSAGE + 1
        f32 = jnp.float32
        whole = pltpu.VMEM((rows, cols), f32)
        small = pltpu.VMEM((8, cols), f32)
        scratch = [
            pltpu.VMEM((3, padded, cols), f32),
            pltpu.VMEM((padded, cols), f32),
            pltpu.VMEM((padded, cols), jnp.int32),
            pltpu.SMEM(owner_table.shape, jnp.int32),
            whole,
            pltpu.VMEM((3, rows, cols), f32),
            whole,
            whole,
            whole,
            whole,
            pltpu.VMEM((32, rows), f32),
            pltpu.VMEM((8, rows), f32),
            pltpu.VMEM((8, rows), f32),
            pltpu.VMEM((4, 16, rows), f32),
            pltpu.VMEM((LANES, rows), f32),
            small,
            pltpu.VMEM((3, 8, cols), f32),
            small,
            small,
            small,
            small,
            pltpu.VMEM((LANES, cols), f32),
            whole,
            pltpu.SemaphoreType.DMA((6,)),
            pltpu.SemaphoreType.DMA((slots,)),
            pltpu.SemaphoreType.DMA((slots,)),
            pltpu.SemaphoreType.DMA((3, slots)),
            pltpu.SemaphoreType.DMA((slots,)),
            pltpu.SemaphoreType.DMA((slots,)),
            pltpu.SemaphoreType.DMA((slots,)),
            pltpu.SemaphoreType.DMA((slots,)),
            pltpu.SemaphoreType.DMA((2,)),
            pltpu.SemaphoreType.DMA((2,)),
        ]
        arrays = [
            pltpu.with_memory_space_constraint(array, pltpu.HBM)
            for array in (fields, friction, wet_mask, owner_table)
        ]
        return pl.pallas_call(
            functools.partial(kernel, axis, count),
            out_shape=(
                jax.ShapeDtypeStruct(fields.shape, f32),
                jax.ShapeDtypeStruct(friction.shape, f32),
            ),
            in_specs=[pl.BlockSpec(memory_space=pltpu.HBM)] * 4,
            out_specs=(
                pl.BlockSpec(memory_space=pltpu.VMEM),
                pl.BlockSpec(memory_space=pltpu.VMEM),
            ),
            scratch_shapes=scratch,
            compiler_params=pltpu.CompilerParams(
                collective_id=0, has_side_effects=True, vmem_limit_bytes=32 * 2**20
            ),
            name="shallow_water",
        )(*arrays)

    in_specs = (P(None, "groups", axis), P("groups", axis), P("groups", axis), P("groups", None))
    out_specs = (P(None, "groups", axis), P("groups", axis))
    return jax.shard_map(body, mesh=mesh, in_specs=in_specs, out_specs=out_specs, check_vma=False)
```

time: 49.6 us -> 47.2 us (0.952)
  local copies, waits for them, and re-layouts: 3.51 us -> 1.94 us
  Pallas kernels: 45.2 us -> 44.5 us
    unnamed x4 -> x2, local copies, waits for them, and re-layouts: 3.51 us -> 1.94 us
    pallas_call x1, Pallas kernels: 45.2 us -> 44.5 us  [body(): pl.pallas_call(functools.partial(kernel, axis, count), out_shape=(jax.Sha...]
where the time goes in v1:
time: 47.2 us; the launch traced here: 47.1 us
  Pallas kernels  44.5 us (94%)
  local copies, waits for them, and re-layouts  1.94 us (4%)
  between operations  0.64 us (1%)
    pallas_call x1, Pallas kernels, body(): pl.pallas_call(functools.partial(kernel, axis, count), out_shape=(jax.Sha...  44.5 us
    unnamed x2, local copies, waits for them, and re-layouts  1.94 us

profile of v1, /device:TPU:513, one launch (start us, length us, event | category | flops | bytes accessed | tf_op | source)
XLA Modules:
  0.0 47.1 jit_solution(12505671415028812943)
XLA Ops:
  0.6 44.5 %shallow_water.1 = (f32[3,512,256]{2,1,0:T(8,128)S(1)}, f32[512,256]{1,0:T(8,128)S(1)}) custom-call(f32[3,512,256]{2,1,0:T(8,128)} %fields_ref.1, f32[512,256]{1,0:T(8,128)} %friction_ref.1, s32[512,256]{1,0:T(8,128)} %wet_ref.1, s32[2,128]{1,0:T(2,128)} %owner_ref.1), custom_call_target="tpu_custom_call" | custom-call | tf_op jit(solution)/shard_map/shallow_water/pallas_call | solution.py:521
  45.1 1.1 %copy.8 = f32[3,512,256]{2,1,0:T(8,128)} copy(f32[3,512,256]{2,1,0:T(8,128)S(1)} %get-tuple-element.4) | data formatting | bytes 3145728
  46.3 0.8 %copy.9 = f32[512,256]{1,0:T(8,128)} copy(f32[512,256]{1,0:T(8,128)S(1)} %get-tuple-element.5) | data formatting | bytes 1048576

commit v2 on v1

--- a/solution.py
+++ b/solution.py
@@ -11,6 +11,8 @@
 PAD = 8
 CHUNK = 64
 MESSAGE = 32
+LAG = 4
+BLOCKS = 4
 LANES = 128
 
 gravity_half = 0.5
@@ -66,6 +68,8 @@
     inbox,
     back,
     turn,
+    near_out,
+    far_out,
     mine,
     other,
     packed,
@@ -82,6 +86,7 @@
     edge_final,
     edge_wide,
     load_sem,
+    table_sem,
     raw_send,
     relay_send,
     in_recv,
@@ -91,11 +96,14 @@
     swap_recv,
     halo_send,
     halo_recv,
+    hello,
 ):
     rows, cols = friction_ref.shape
     tile = cols
     tile_rows = rows // tile
     messages = rows // MESSAGE
+    half = messages // 2
+    chunks = rows // CHUNK
     extra = messages
     MESH = pl.DeviceIdType.MESH
 
@@ -107,6 +115,9 @@
     toward = me + 2 - 4 * (chip // 2)
     outward = 2 * me - toward
     sibling = me + 1 - 2 * odd
+    is_first = chip == 0
+    is_third = chip == 2
+    swapped = chip // 3
     is_middle = middle == 1
     is_end = middle == 0
 
@@ -116,17 +127,38 @@
     lead_right = jnp.where(position == 7, 1, 1 - odd) * (1 - last)
     follow_right = (1 - last) * (1 - lead_right)
 
-    loads = [
-        pltpu.make_async_copy(
-            fields_ref.at[plane], state.at[plane, pl.ds(PAD, rows), :], load_sem.at[plane]
-        )
-        for plane in range(3)
-    ]
-    loads.append(pltpu.make_async_copy(friction_ref, fric.at[pl.ds(PAD, rows), :], load_sem.at[3]))
-    loads.append(pltpu.make_async_copy(wet_ref, mask.at[pl.ds(PAD, rows), :], load_sem.at[4]))
-    loads.append(pltpu.make_async_copy(owner_ref, owner, load_sem.at[5]))
-    for load in loads:
-        load.start()
+    height = rows // BLOCKS
+
+    def load(number):
+        block = lax.rem(number + swapped, BLOCKS)
+        start = pl.multiple_of(block * height, height)
+        here = pl.ds(start, height)
+        there = pl.ds(start + PAD, height)
+        copies = [
+            pltpu.make_async_copy(
+                fields_ref.at[plane, here, :],
+                state.at[plane, there, :],
+                load_sem.at[number, plane],
+            )
+            for plane in range(3)
+        ]
+        copies.append(
+            pltpu.make_async_copy(friction_ref.at[here, :], fric.at[there, :], load_sem.at[number, 3])
+        )
+        copies.append(
+            pltpu.make_async_copy(wet_ref.at[here, :], mask.at[there, :], load_sem.at[number, 4])
+        )
+        return copies
+
+    def await_load(number):
+        for copy in load(number):
+            copy.wait()
+
+    table = pltpu.make_async_copy(owner_ref, owner, table_sem)
+    for number in range(BLOCKS):
+        for copy in load(number):
+            copy.start()
+    table.start()
 
     barrier = pltpu.get_barrier_semaphore()
 
@@ -137,6 +169,10 @@
     def _():
         greet(outward)
         greet(toward)
+
+    @pl.when(is_third)
+    def _():
+        greet(me - 4)
 
     @pl.when(follow_left == 1)
     def _():
@@ -186,6 +222,21 @@
     def give(m):
         return remote(turn.at[span(m), :], back.at[span(m), :], back_send.at[m], back_recv.at[m], outward)
 
+    def give_raw(m):
+        return remote(
+            first.at[span(m), :], back.at[span(m), :], back_send.at[m], back_recv.at[m], outward
+        )
+
+    def near_direct(m):
+        return remote(
+            near_out.at[span(m), :], inbox.at[1, span(m), :], raw_send.at[m], in_recv.at[1, m], me - 2
+        )
+
+    def far_direct(m):
+        return remote(
+            far_out.at[span(m), :], inbox.at[2, span(m), :], relay_send.at[m], in_recv.at[2, m], me - 4
+        )
+
     def swap(m):
         return remote(mine.at[span(m), :], other.at[span(m), :], swap_send.at[m], swap_recv.at[m], sibling)
 
@@ -209,9 +260,9 @@
         return lambda a: pltpu.roll(a, amount % size, axis_number)
 
     def compute(i):
-        height = CHUNK + 2 * PAD
+        reach = CHUNK + 2 * PAD
         at = pl.multiple_of(i * CHUNK, CHUNK)
-        where = pl.ds(at, height)
+        where = pl.ds(at, reach)
         openness = mask[where, :].astype(jnp.float32) * fric[where, :]
         wet, damping = masks(openness)
         values = tuple(state[plane, where, :] * wet for plane in range(3))
@@ -222,21 +273,57 @@
                 damping,
                 shift(1, -1, cols),
                 shift(1, 1, cols),
-                shift(0, -1, height),
-                shift(0, 1, height),
+                shift(0, -1, reach),
+                shift(0, 1, reach),
             )
         here = pl.ds(at, CHUNK)
         first[here, :] = values[0][PAD : PAD + CHUNK]
         for plane in range(3):
             out_fields[plane, here, :] = values[plane][PAD : PAD + CHUNK]
 
-    for load in loads:
-        load.wait()
-
-    compute(0)
-    pl.semaphore_wait(barrier, 1 + lead_left + lead_right)
-    for part in range(CHUNK // MESSAGE):
-        raw(part, middle).start()
+    def for_end(by, own, near, far):
+        return jnp.where(by == 3, far, jnp.where(by == 2, near, own))
+
+    def for_middle(by, own, end, near, far):
+        return jnp.where(by == 3, near, jnp.where(by == 2, far, jnp.where(by == 1, end, own)))
+
+    def of_row(pair, m, shape):
+        value = pair[-1]
+        for tile_row in reversed(range(tile_rows - 1)):
+            value = jnp.where(m < (tile_row + 1) * (tile // MESSAGE), pair[tile_row], value)
+        return jnp.full(shape, value, jnp.int32)
+
+    def send_chunk(number):
+        for part in range(CHUNK // MESSAGE):
+            raw(number * (CHUNK // MESSAGE) + part, middle).start()
+
+    def chunk_at(j):
+        return lax.rem(j + swapped * (chunks // 2), chunks)
+
+    await_load(0)
+
+    @pl.when(swapped == 1)
+    def _():
+        await_load(1)
+
+    compute(chunk_at(0))
+    pl.semaphore_wait(barrier, 1 + lead_left + lead_right + jnp.where(is_first, 1, 0))
+    send_chunk(chunk_at(0))
+
+    @pl.when(is_first)
+    def _():
+        for peer in (me + 2, me + 4):
+            pl.semaphore_signal(hello, inc=1, device_id={axis: peer}, device_id_type=MESH)
+
+    @pl.when(swapped == 0)
+    def _():
+        await_load(1)
+
+    for number in range(2, BLOCKS):
+        await_load(number)
+    table.wait()
+    moves = [differs(tile_row, 1) + 2 * differs(tile_row, 2) for tile_row in range(tile_rows)]
+    flips = [differs(tile_row, 0) for tile_row in range(tile_rows)]
 
     lane = lax.broadcasted_iota(jnp.int32, (LANES, LANES), 1)
 
@@ -265,11 +352,13 @@
     def _():
         halo_to_right.start()
 
-    @pl.loop(1, rows // CHUNK)
-    def _(i):
-        compute(i)
-        for part in range(CHUNK // MESSAGE):
-            raw(i * (CHUNK // MESSAGE) + part, middle).start()
+    @pl.loop(1, chunks)
+    def _(j):
+        compute(chunk_at(j))
+
+        @pl.when((chip != 2) | (j < chunks // 2))
+        def _():
+            send_chunk(chunk_at(j))
 
     @pl.when(follow_right == 1)
     def _():
@@ -280,6 +369,24 @@
     def _():
         halo_to_right.wait_recv()
         halo_to_left.start()
+
+    @pl.when(is_third)
+    def _():
+        @pl.loop(half, messages)
+        def _(m):
+            raw(m, 0).wait_recv()
+            where = span(m)
+            by = of_row(moves, m, (MESSAGE, cols))
+            near_out[where, :] = jnp.where(by == 3, first[where, :], inbox[0, where, :])
+            near_direct(m).start()
+
+    @pl.when(chip == 1)
+    def _():
+        pl.semaphore_wait(hello, 1)
+
+        @pl.loop(half, messages)
+        def _(m):
+            give_raw(m).start()
 
     @pl.when(lead_right == 1)
     def _():
@@ -319,18 +426,58 @@
         edge_first[4 * tile_row + 2 : 4 * tile_row + 4, :] = edge_turn[10:12, cut]
     edge_raw(middle).start()
 
-    @pl.when(is_middle)
-    def _():
-        @pl.loop(0, messages - 2)
-        def _(m):
-            raw(m, 0).wait_recv()
-            relay(m).start()
+    def settle_second(m, late):
+        where = span(m)
+        by = of_row(moves, m, (MESSAGE, cols))
+        raw(m, 1).wait_recv()
+        own = first[where, :]
+        end = inbox[0, where, :]
+        near = inbox[1, where, :]
+        if late:
+            mine[where, :] = jnp.where(by >= 2, near, jnp.where(by == 1, end, own))
+        else:
+            relay(m).wait_recv()
+            far = inbox[2, where, :]
+            turn[where, :] = for_end(by, own, near, far)
+            give(m).start()
+            mine[where, :] = for_middle(by, own, end, near, far)
+        swap(m).start()
+
+    def pass_on(m):
+        raw(m, 0).wait_recv()
+        relay(m).start()
+
+    @pl.when(is_third)
+    def _():
+        @pl.loop(0, half)
+        def _(m):
+            pass_on(m)
 
         edge_raw(0).wait_recv()
         edge_relay.start()
-        for m in range(messages - 2, messages):
-            raw(m, 0).wait_recv()
-            relay(m).start()
+        pl.semaphore_wait(hello, 1)
+
+        @pl.loop(half, messages)
+        def _(m):
+            where = span(m)
+            by = of_row(moves, m, (MESSAGE, cols))
+            far_out[where, :] = jnp.where(by == 2, first[where, :], inbox[0, where, :])
+            far_direct(m).start()
+
+    @pl.when(chip == 1)
+    def _():
+        for m in range(LAG):
+            pass_on(m)
+
+        @pl.loop(0, half)
+        def _(m):
+            settle_second(m, False)
+            pass_on(m + LAG)
+
+        for m in range(half + LAG, messages):
+            pass_on(m)
+        edge_raw(0).wait_recv()
+        edge_relay.start()
 
     @pl.loop(0, rows // LANES)
     def _(block):
@@ -348,26 +495,11 @@
                 lane >= LANES - 2, on_right, out_fields[plane, where, cut]
             )
 
-    moves = [differs(tile_row, 1) + 2 * differs(tile_row, 2) for tile_row in range(tile_rows)]
-    flips = [differs(tile_row, 0) for tile_row in range(tile_rows)]
-
-    def for_end(by, own, near, far):
-        return jnp.where(by == 3, far, jnp.where(by == 2, near, own))
-
-    def for_middle(by, own, end, near, far):
-        return jnp.where(by == 3, near, jnp.where(by == 2, far, jnp.where(by == 1, end, own)))
-
-    def of_row(pair, m, shape):
-        value = pair[-1]
-        for tile_row in reversed(range(tile_rows - 1)):
-            value = jnp.where(m < (tile_row + 1) * (tile // MESSAGE), pair[tile_row], value)
-        return jnp.full(shape, value, jnp.int32)
-
-    def settle(m):
+    def settle(m, late):
         where = span(m)
         by = of_row(moves, m, (MESSAGE, cols))
 
-        @pl.when(is_middle)
+        @pl.when(is_third)
         def _():
             raw(m, 1).wait_recv()
             relay(m).wait_recv()
@@ -381,6 +513,17 @@
         @pl.when(is_end)
         def _():
             give(m).wait_recv()
+
+        @pl.when(is_first)
+        def _():
+            taken = back[where, :]
+            if late:
+                relay(m).wait_recv()
+                taken = jnp.where(by >= 2, inbox[2, where, :], taken)
+            mine[where, :] = jnp.where(by == 0, first[where, :], taken)
+
+        @pl.when(chip == 3)
+        def _():
             mine[where, :] = jnp.where(by == 0, first[where, :], back[where, :])
 
         swap(m).start()
@@ -393,9 +536,11 @@
             value = jnp.where(line < 4 * (tile_row + 1), pair[tile_row], value)
         return value
 
-    @pl.loop(0, messages - 2)
-    def _(m):
-        settle(m)
+    @pl.when(chip != 1)
+    def _():
+        @pl.loop(0, half)
+        def _(m):
+            settle(m, False)
 
     edge_by = by_line(moves)
 
@@ -416,8 +561,18 @@
         edge_mine[...] = jnp.where(edge_by == 0, edge_first[...], edge_back[...])
 
     edge_swap.start()
-    for m in range(messages - 2, messages):
-        settle(m)
+
+    @pl.when(chip != 1)
+    def _():
+        @pl.loop(half, messages)
+        def _(m):
+            settle(m, True)
+
+    @pl.when(chip == 1)
+    def _():
+        @pl.loop(half, messages)
+        def _(m):
+            settle_second(m, True)
 
     edge_swap.wait_recv()
     edge_final[0:8, :] = jnp.where(by_line(flips) == 1, edge_other[...], edge_mine[...])
@@ -490,6 +645,8 @@
             whole,
             whole,
             whole,
+            whole,
+            whole,
             pltpu.VMEM((32, rows), f32),
             pltpu.VMEM((8, rows), f32),
             pltpu.VMEM((8, rows), f32),
@@ -503,7 +660,8 @@
             small,
             pltpu.VMEM((LANES, cols), f32),
             whole,
-            pltpu.SemaphoreType.DMA((6,)),
+            pltpu.SemaphoreType.DMA((BLOCKS, 5)),
+            pltpu.SemaphoreType.DMA,
             pltpu.SemaphoreType.DMA((slots,)),
             pltpu.SemaphoreType.DMA((slots,)),
             pltpu.SemaphoreType.DMA((3, slots)),
@@ -513,6 +671,7 @@
             pltpu.SemaphoreType.DMA((slots,)),
             pltpu.SemaphoreType.DMA((2,)),
             pltpu.SemaphoreType.DMA((2,)),
+            pltpu.SemaphoreType.REGULAR,
         ]
         arrays = [
             pltpu.with_memory_space_constraint(array, pltpu.HBM)

time: 47.2 us -> 44.9 us (0.951)
  Pallas kernels: 44.5 us -> 42.2 us
    pallas_call x1, Pallas kernels: 44.5 us -> 42.2 us  [body(): pl.pallas_call(functools.partial(kernel, axis, count), out_shape=(jax.Sha...]
where the time goes in v2:
time: 44.9 us; the launch traced here: 44.8 us
  Pallas kernels  42.2 us (94%)
  local copies, waits for them, and re-layouts  1.94 us (4%)
  between operations  0.64 us (1%)
    pallas_call x1, Pallas kernels, body(): pl.pallas_call(functools.partial(kernel, axis, count), out_shape=(jax.Sha...  42.2 us
    unnamed x2, local copies, waits for them, and re-layouts  1.94 us

profile of v2, /device:TPU:513, one launch (start us, length us, event | category | flops | bytes accessed | tf_op | source)
XLA Modules:
  0.0 44.8 jit_solution(15574718856788915518)
XLA Ops:
  0.6 42.2 %shallow_water.1 = (f32[3,512,256]{2,1,0:T(8,128)S(1)}, f32[512,256]{1,0:T(8,128)S(1)}) custom-call(f32[3,512,256]{2,1,0:T(8,128)} %fields_ref.1, f32[512,256]{1,0:T(8,128)} %friction_ref.1, s32[512,256]{1,0:T(8,128)} %wet_ref.1, s32[2,128]{1,0:T(2,128)} %owner_ref.1), custom_call_target="tpu_custom_call" | custom-call | tf_op jit(solution)/shard_map/shallow_water/pallas_call | solution.py:680
  42.9 1.1 %copy.8 = f32[3,512,256]{2,1,0:T(8,128)} copy(f32[3,512,256]{2,1,0:T(8,128)S(1)} %get-tuple-element.4) | data formatting | bytes 3145728
  44.0 0.8 %copy.9 = f32[512,256]{1,0:T(8,128)} copy(f32[512,256]{1,0:T(8,128)S(1)} %get-tuple-element.5) | data formatting | bytes 1048576

commit v3 on v2

--- a/solution.py
+++ b/solution.py
@@ -117,23 +117,22 @@
     sibling = me + 1 - 2 * odd
     is_first = chip == 0
     is_third = chip == 2
-    swapped = chip // 3
     is_middle = middle == 1
     is_end = middle == 0
 
     last = jnp.where(me == count - 1, 1, 0)
-    lead_left = jnp.where(position == 0, 0, 1 - odd)
+    parity = (me // 8) % 2
+    lead_left = jnp.where(position == 0, parity, jnp.where(position == 6, 1, 0))
+    lead_left = jnp.where(me == 0, 0, lead_left)
     follow_left = jnp.where(me == 0, 0, 1 - lead_left)
-    lead_right = jnp.where(position == 7, 1, 1 - odd) * (1 - last)
+    lead_right = jnp.where(position == 7, parity, jnp.where(position == 5, 0, 1)) * (1 - last)
     follow_right = (1 - last) * (1 - lead_right)
 
     height = rows // BLOCKS
 
     def load(number):
-        block = lax.rem(number + swapped, BLOCKS)
-        start = pl.multiple_of(block * height, height)
-        here = pl.ds(start, height)
-        there = pl.ds(start + PAD, height)
+        here = pl.ds(number * height, height)
+        there = pl.ds(number * height + PAD, height)
         copies = [
             pltpu.make_async_copy(
                 fields_ref.at[plane, here, :],
@@ -297,29 +296,17 @@
         for part in range(CHUNK // MESSAGE):
             raw(number * (CHUNK // MESSAGE) + part, middle).start()
 
-    def chunk_at(j):
-        return lax.rem(j + swapped * (chunks // 2), chunks)
-
     await_load(0)
-
-    @pl.when(swapped == 1)
-    def _():
-        await_load(1)
-
-    compute(chunk_at(0))
+    compute(0)
     pl.semaphore_wait(barrier, 1 + lead_left + lead_right + jnp.where(is_first, 1, 0))
-    send_chunk(chunk_at(0))
+    send_chunk(0)
 
     @pl.when(is_first)
     def _():
         for peer in (me + 2, me + 4):
             pl.semaphore_signal(hello, inc=1, device_id={axis: peer}, device_id_type=MESH)
 
-    @pl.when(swapped == 0)
-    def _():
-        await_load(1)
-
-    for number in range(2, BLOCKS):
+    for number in range(1, BLOCKS):
         await_load(number)
     table.wait()
     moves = [differs(tile_row, 1) + 2 * differs(tile_row, 2) for tile_row in range(tile_rows)]
@@ -354,11 +341,11 @@
 
     @pl.loop(1, chunks)
     def _(j):
-        compute(chunk_at(j))
+        compute(j)
 
         @pl.when((chip != 2) | (j < chunks // 2))
         def _():
-            send_chunk(chunk_at(j))
+            send_chunk(j)
 
     @pl.when(follow_right == 1)
     def _():
@@ -370,8 +357,16 @@
         halo_to_right.wait_recv()
         halo_to_left.start()
 
+    def pass_on(m):
+        raw(m, 0).wait_recv()
+        relay(m).start()
+
     @pl.when(is_third)
     def _():
+        @pl.loop(0, half)
+        def _(m):
+            pass_on(m)
+
         @pl.loop(half, messages)
         def _(m):
             raw(m, 0).wait_recv()
@@ -443,16 +438,8 @@
             mine[where, :] = for_middle(by, own, end, near, far)
         swap(m).start()
 
-    def pass_on(m):
-        raw(m, 0).wait_recv()
-        relay(m).start()
-
     @pl.when(is_third)
     def _():
-        @pl.loop(0, half)
-        def _(m):
-            pass_on(m)
-
         edge_raw(0).wait_recv()
         edge_relay.start()
         pl.semaphore_wait(hello, 1)
@@ -544,23 +531,28 @@
 
     edge_by = by_line(moves)
 
-    @pl.when(is_middle)
-    def _():
-        edge_raw(1).wait_recv()
-        edge_relay.wait_recv()
-        own = edge_first[...]
-        near = edge_in[1]
-        far = edge_in[2]
-        edge_give[...] = for_end(edge_by, own, near, far)
-        edge_return.start()
-        edge_mine[...] = for_middle(edge_by, own, edge_in[0], near, far)
-
-    @pl.when(is_end)
-    def _():
-        edge_return.wait_recv()
-        edge_mine[...] = jnp.where(edge_by == 0, edge_first[...], edge_back[...])
-
-    edge_swap.start()
+    def settle_edges():
+        @pl.when(is_middle)
+        def _():
+            edge_raw(1).wait_recv()
+            edge_relay.wait_recv()
+            own = edge_first[...]
+            near = edge_in[1]
+            far = edge_in[2]
+            edge_give[...] = for_end(edge_by, own, near, far)
+            edge_return.start()
+            edge_mine[...] = for_middle(edge_by, own, edge_in[0], near, far)
+
+        @pl.when(is_end)
+        def _():
+            edge_return.wait_recv()
+            edge_mine[...] = jnp.where(edge_by == 0, edge_first[...], edge_back[...])
+
+        edge_swap.start()
+
+    @pl.when(chip < 2)
+    def _():
+        settle_edges()
 
     @pl.when(chip != 1)
     def _():
@@ -573,6 +565,10 @@
         @pl.loop(half, messages)
         def _(m):
             settle_second(m, True)
+
+    @pl.when(chip >= 2)
+    def _():
+        settle_edges()
 
     edge_swap.wait_recv()
     edge_final[0:8, :] = jnp.where(by_line(flips) == 1, edge_other[...], edge_mine[...])

time: 44.9 us -> 42.8 us (0.953)
  Pallas kernels: 42.2 us -> 40.1 us
    pallas_call x1, Pallas kernels: 42.2 us -> 40.1 us  [body(): pl.pallas_call(functools.partial(kernel, axis, count), out_shape=(jax.Sha...]
where the time goes in v3:
time: 42.8 us; the launch traced here: 42.6 us
  Pallas kernels  40.1 us (94%)
  local copies, waits for them, and re-layouts  1.94 us (5%)
  between operations  0.64 us (1%)
    pallas_call x1, Pallas kernels, body(): pl.pallas_call(functools.partial(kernel, axis, count), out_shape=(jax.Sha...  40.1 us
    unnamed x2, local copies, waits for them, and re-layouts  1.94 us

profile of v3, /device:TPU:513, one launch (start us, length us, event | category | flops | bytes accessed | tf_op | source)
XLA Modules:
  0.0 42.6 jit_solution(13052274072154238084)
XLA Ops:
  0.6 40.1 %shallow_water.1 = (f32[3,512,256]{2,1,0:T(8,128)S(1)}, f32[512,256]{1,0:T(8,128)S(1)}) custom-call(f32[3,512,256]{2,1,0:T(8,128)} %fields_ref.1, f32[512,256]{1,0:T(8,128)} %friction_ref.1, s32[512,256]{1,0:T(8,128)} %wet_ref.1, s32[2,128]{1,0:T(2,128)} %owner_ref.1), custom_call_target="tpu_custom_call" | custom-call | tf_op jit(solution)/shard_map/shallow_water/pallas_call | solution.py:676
  40.7 1.1 %copy.8 = f32[3,512,256]{2,1,0:T(8,128)} copy(f32[3,512,256]{2,1,0:T(8,128)S(1)} %get-tuple-element.4) | data formatting | bytes 3145728
  41.9 0.8 %copy.9 = f32[512,256]{1,0:T(8,128)} copy(f32[512,256]{1,0:T(8,128)S(1)} %get-tuple-element.5) | data formatting | bytes 1048576

commit v4 on v3

v4 whole, which is shorter than its diff:
```python
import functools

import jax
import jax.numpy as jnp
from jax import lax
from jax.experimental import pallas as pl
from jax.experimental.pallas import tpu as pltpu
from jax.sharding import PartitionSpec as P

STEPS = 2
PAD = 8
CHUNK = 64
MESSAGE = 32
LAG = 8
AHEAD = 6
DIRECT = 4
FIRST = 128
LANES = 128

gravity_half = 0.5
depth_floor = 0.25
flux_factor = 0.1
time_step = 0.25


def advance(state, wet, damping, east, west, south, north):
    h, p, q = state
    inverse = 1.0 / jnp.maximum(h, depth_floor)
    u = p * inverse
    v = q * inverse
    pressure = gravity_half * h * h
    cross = q * u
    flux_p = p * u + pressure
    flux_q = q * v + pressure

    def gather(cell, flux_east, flux_south):
        quarter = 0.25 * cell
        along = flux_factor * flux_east
        down = flux_factor * flux_south
        return (east(quarter - along) + west(quarter + along)) + (
            south(quarter - down) + north(quarter + down)
        )

    return (
        wet * gather(h, p, q),
        damping * gather(p, flux_p, cross),
        damping * gather(q, cross, flux_q),
    )


def masks(openness):
    wet = jnp.where(openness > 0.0, 1.0, 0.0)
    return wet, wet / (1.0 + time_step * openness)


def kernel(
    axis,
    count,
    fields_ref,
    friction_ref,
    wet_ref,
    owner_ref,
    out_fields,
    out_depth,
    state,
    fric,
    mask,
    owner,
    first,
    inbox,
    back,
    turn,
    near_out,
    far_out,
    mine,
    other,
    packed,
    halo_left,
    halo_right,
    edge,
    edge_turn,
    edge_first,
    edge_in,
    edge_back,
    edge_give,
    edge_near,
    edge_mine,
    edge_other,
    edge_final,
    edge_wide,
    load_sem,
    table_sem,
    raw_send,
    relay_send,
    in_recv,
    back_send,
    swap_send,
    swap_recv,
    halo_send,
    halo_recv,
    hello,
):
    rows, cols = friction_ref.shape
    tile = cols
    tile_rows = rows // tile
    messages = rows // MESSAGE
    split = messages - DIRECT
    chunks = rows // CHUNK
    extra = messages
    MESH = pl.DeviceIdType.MESH

    me = lax.axis_index(axis)
    odd = me % 2
    position = me % 8
    chip = position // 2
    middle = ((chip + 1) // 2) % 2
    toward = me + 2 - 4 * (chip // 2)
    outward = 2 * me - toward
    sibling = me + 1 - 2 * odd
    keeper = me - position + 1
    is_keeper = position == 1
    is_leaf = position == 0
    is_third = chip == 2
    is_middle = middle == 1
    is_end = middle == 0

    last = jnp.where(me == count - 1, 1, 0)
    parity = (me // 8) % 2
    lead_left = jnp.where(position == 0, parity, jnp.where(position == 6, 1, 0))
    lead_left = jnp.where(me == 0, 0, lead_left)
    follow_left = jnp.where(me == 0, 0, 1 - lead_left)
    lead_right = jnp.where(position == 7, parity, jnp.where(position == 5, 0, 1)) * (1 - last)
    follow_right = (1 - last) * (1 - lead_right)

    def load(number):
        start, size = ((0, FIRST), (FIRST, rows - FIRST))[number]
        here = pl.ds(start, size)
        there = pl.ds(start + PAD, size)
        return [
            pltpu.make_async_copy(
                fields_ref.at[:, here, :], state.at[:, there, :], load_sem.at[number, 0]
            ),
            pltpu.make_async_copy(friction_ref.at[here, :], fric.at[there, :], load_sem.at[number, 1]),
            pltpu.make_async_copy(wet_ref.at[here, :], mask.at[there, :], load_sem.at[number, 2]),
        ]

    def await_load(number):
        for copy in load(number):
            copy.wait()

    table = pltpu.make_async_copy(owner_ref, owner, table_sem)
    for number in range(2):
        for copy in load(number):
            copy.start()
    table.start()

    barrier = pltpu.get_barrier_semaphore()

    def greet(peer):
        pl.semaphore_signal(barrier, inc=1, device_id={axis: peer}, device_id_type=MESH)

    @pl.when(is_middle)
    def _():
        greet(outward)
        greet(toward)

    @pl.when(is_third)
    def _():
        greet(keeper)

    @pl.when(follow_left == 1)
    def _():
        greet(me - 1)

    @pl.when(follow_right == 1)
    def _():
        greet(me + 1)

    zero_rows = jnp.zeros((PAD, cols), jnp.float32)
    for start in (0, PAD + rows):
        for plane in range(3):
            state[plane, start : start + PAD, :] = zero_rows
        fric[start : start + PAD, :] = zero_rows
        mask[start : start + PAD, :] = jnp.zeros((PAD, cols), jnp.int32)
    edge[...] = jnp.zeros_like(edge)
    edge_turn[...] = jnp.zeros_like(edge_turn)
    edge_final[...] = jnp.zeros_like(edge_final)

    def differs(tile_row, bit):
        own = owner[tile_row, me]
        return (own // 2 ** bit + me // 2 ** bit) % 2

    def remote(src, dst, send, recv, peer):
        return pltpu.make_async_remote_copy(
            src_ref=src,
            dst_ref=dst,
            send_sem=send,
            recv_sem=recv,
            device_id={axis: peer},
            device_id_type=MESH,
        )

    def span(m):
        return pl.ds(pl.multiple_of(m * MESSAGE, MESSAGE), MESSAGE)

    def raw(m, slot):
        return remote(
            first.at[span(m), :], inbox.at[slot, span(m), :], raw_send.at[0], in_recv.at[slot, m], toward
        )

    def relay(m):
        return remote(
            inbox.at[0, span(m), :], inbox.at[2, span(m), :], relay_send.at[0], in_recv.at[2, m], toward
        )

    plane_slot = jnp.where(chip == 1, odd, 0)
    receiver = jnp.where(chip == 1, keeper, outward)

    def give(m, source, slot):
        return remote(
            source.at[span(m), :],
            back.at[slot, span(m), :],
            back_send.at[0],
            in_recv.at[slot, m],
            receiver,
        )

    def near_direct(m):
        return remote(
            near_out.at[span(m), :], inbox.at[1, span(m), :], raw_send.at[0], in_recv.at[1, m], me - 2
        )

    def far_direct(m, core):
        return remote(
            far_out.at[span(m), :],
            inbox.at[1 + core, span(m), :],
            relay_send.at[0],
            in_recv.at[2, m - (1 - core) * split],
            keeper,
        )

    def pass_back(m, slot):
        return remote(
            near_out.at[span(m), :], other.at[span(m), :], swap_send.at[0], swap_recv.at[slot], sibling
        )

    def swap(m, slot):
        return remote(
            mine.at[span(m), :], other.at[span(m), :], swap_send.at[0], swap_recv.at[slot], sibling
        )

    def edge_raw(slot):
        return remote(edge_first, edge_in.at[slot], raw_send.at[1], in_recv.at[slot, extra], toward)

    edge_relay = remote(
        edge_in.at[0], edge_in.at[2], relay_send.at[1], in_recv.at[2, extra], toward
    )

    def edge_return(slot):
        return remote(
            edge_give, edge_back.at[slot], back_send.at[1], in_recv.at[slot, extra], receiver
        )

    edge_pass = remote(edge_near, edge_other, swap_send.at[1], swap_recv.at[1], sibling)
    edge_swap = remote(edge_mine, edge_other, swap_send.at[1], swap_recv.at[1], sibling)

    halo_to_left = remote(
        packed.at[pl.ds(0, 16), :], halo_right, halo_send.at[0], halo_recv.at[0], me - 1
    )
    halo_to_right = remote(
        packed.at[pl.ds(16, 16), :], halo_left, halo_send.at[1], halo_recv.at[1], me + 1
    )

    def shift(axis_number, amount, size):
        return lambda a: pltpu.roll(a, amount % size, axis_number)

    def compute(i):
        reach = CHUNK + 2 * PAD
        at = pl.multiple_of(i * CHUNK, CHUNK)
        where = pl.ds(at, reach)
        openness = mask[where, :].astype(jnp.float32) * fric[where, :]
        wet, damping = masks(openness)
        values = tuple(state[plane, where, :] * wet for plane in range(3))
        for _ in range(STEPS):
            values = advance(
                values,
                wet,
                damping,
                shift(1, -1, cols),
                shift(1, 1, cols),
                shift(0, -1, reach),
                shift(0, 1, reach),
            )
        here = pl.ds(at, CHUNK)
        first[here, :] = values[0][PAD : PAD + CHUNK]
        for plane in range(3):
            out_fields[plane, here, :] = values[plane][PAD : PAD + CHUNK]

    def for_end(by, own, near, far):
        return jnp.where(by == 3, far, jnp.where(by == 2, near, own))

    def for_middle(by, own, end, near, far):
        return jnp.where(by == 3, near, jnp.where(by == 2, far, jnp.where(by == 1, end, own)))

    def of_row(pair, m, shape):
        value = pair[-1]
        for tile_row in reversed(range(tile_rows - 1)):
            value = jnp.where(m < (tile_row + 1) * (tile // MESSAGE), pair[tile_row], value)
        return jnp.full(shape, value, jnp.int32)

    def send_chunk(number):
        for part in range(CHUNK // MESSAGE):
            raw(number * (CHUNK // MESSAGE) + part, middle).start()

    @pl.when(is_keeper)
    def _():
        pl.semaphore_wait(barrier, 3 + lead_left + lead_right)
        for ahead in range(1, 5):
            pl.semaphore_signal(hello, inc=1, device_id={axis: me + ahead}, device_id_type=MESH)

    await_load(0)
    compute(0)

    @pl.when(position != 1)
    def _():
        pl.semaphore_wait(barrier, 1 + lead_left + lead_right)

    send_chunk(0)
    await_load(1)
    table.wait()
    moves = [differs(tile_row, 1) + 2 * differs(tile_row, 2) for tile_row in range(tile_rows)]
    flips = [differs(tile_row, 0) for tile_row in range(tile_rows)]

    compute(1)
    send_chunk(1)

    lane = lax.broadcasted_iota(jnp.int32, (LANES, LANES), 1)

    @pl.loop(0, rows // LANES)
    def _(block):
        where = pl.ds(pl.multiple_of(PAD + block * LANES, PAD), LANES)
        result = jnp.zeros((LANES, LANES), jnp.float32)
        for side, low in enumerate((0, cols - LANES)):
            cut = pl.ds(low, LANES)
            openness = mask[where, cut].astype(jnp.float32) * fric[where, cut]
            wet = jnp.where(openness > 0.0, 1.0, 0.0)
            planes = [state[plane, where, cut] * wet for plane in range(3)] + [openness]
            for number, values in enumerate(planes):
                source = (LANES - 4) * side
                target = 16 * side + 4 * number
                moved = pltpu.roll(values, (target - source) % LANES, 1)
                result = jnp.where(lane >= target, moved, result)
        packed[:, pl.ds(pl.multiple_of(block * LANES, LANES), LANES)] = result.T[0:32]

    @pl.when(lead_left == 1)
    def _():
        halo_to_left.start()

    @pl.when(lead_right == 1)
    def _():
        halo_to_right.start()

    @pl.loop(2, chunks)
    def _(j):
        compute(j)

        @pl.when((chip != 2) | (j < split * MESSAGE // CHUNK))
        def _():
            send_chunk(j)

    @pl.when(follow_right == 1)
    def _():
        halo_to_left.wait_recv()
        halo_to_right.start()

    @pl.when(follow_left == 1)
    def _():
        halo_to_right.wait_recv()
        halo_to_left.start()

    def pass_on(m):
        raw(m, 0).wait_recv()
        relay(m).start()

    @pl.when(is_third)
    def _():
        @pl.loop(0, split)
        def _(m):
            pass_on(m)

        @pl.loop(split, messages)
        def _(m):
            raw(m, 0).wait_recv()
            where = span(m)
            by = of_row(moves, m, (MESSAGE, cols))
            near_out[where, :] = jnp.where(by == 3, first[where, :], inbox[0, where, :])
            near_direct(m).start()

    @pl.when(chip == 1)
    def _():
        pl.semaphore_wait(hello, 1)

        @pl.loop(split, messages)
        def _(m):
            give(m, first, plane_slot).start()

    @pl.when(lead_right == 1)
    def _():
        halo_to_left.wait_recv()

    @pl.when(lead_left == 1)
    def _():
        halo_to_right.wait_recv()

    for number in range(4):
        base = 4 * number
        edge[number, 0:2, :] = jnp.where(me > 0, halo_left[base + 2 : base + 4, :], 0.0)
        edge[number, 2:6, :] = packed[base : base + 4, :]
        edge[number, 8:12, :] = packed[16 + base : 20 + base, :]
        edge[number, 12:14, :] = jnp.where(me < count - 1, halo_right[base : base + 2, :], 0.0)

    place = lax.broadcasted_iota(jnp.int32, (16, rows), 1)
    wet, damping = masks(edge[3])
    values = tuple(edge[plane] for plane in range(3))
    for _ in range(STEPS):
        values = advance(
            values,
            wet,
            damping,
            shift(0, -1, 16),
            shift(0, 1, 16),
            lambda a: jnp.where(place == rows - 1, 0.0, pltpu.roll(a, rows - 1, 1)),
            lambda a: jnp.where(place == 0, 0.0, pltpu.roll(a, 1, 1)),
        )
    for plane in range(3):
        edge_turn[16 * plane : 16 * plane + 16, :] = values[plane]
    for tile_row in range(tile_rows):
        cut = pl.ds(tile_row * tile, tile)
        edge_first[4 * tile_row : 4 * tile_row + 2, :] = edge_turn[2:4, cut]
        edge_first[4 * tile_row + 2 : 4 * tile_row + 4, :] = edge_turn[10:12, cut]
    edge_raw(middle).start()

    line = lax.broadcasted_iota(jnp.int32, (8, cols), 0)

    def by_line(pair):
        value = jnp.full((8, cols), pair[-1], jnp.int32)
        for tile_row in reversed(range(tile_rows - 1)):
            value = jnp.where(line < 4 * (tile_row + 1), pair[tile_row], value)
        return value

    edge_by = by_line(moves)

    def return_second(m):
        where = span(m)
        by = of_row(moves, m, (MESSAGE, cols))
        raw(m, 1).wait_recv()
        relay(m).wait_recv()
        turn[where, :] = for_end(by, first[where, :], inbox[1, where, :], inbox[2, where, :])
        give(m, turn, plane_slot).start()

    def settle_second(m, late):
        where = span(m)
        by = of_row(moves, m, (MESSAGE, cols))
        if late:
            raw(m, 1).wait_recv()
        own = first[where, :]
        end = inbox[0, where, :]
        near = inbox[1, where, :]
        if late:
            mine[where, :] = jnp.where(by >= 2, near, jnp.where(by == 1, end, own))
        else:
            mine[where, :] = for_middle(by, own, end, near, inbox[2, where, :])
        swap(m, m - split + 2 if late else 0).start()

    @pl.when(is_third)
    def _():
        edge_raw(0).wait_recv()
        edge_relay.start()
        pl.semaphore_wait(hello, 1)

        @pl.loop(split, messages)
        def _(m):
            where = span(m)
            by = of_row(moves, m, (MESSAGE, cols))
            far_out[where, :] = jnp.where(by == 2, first[where, :], inbox[0, where, :])
            far_direct(m, odd).start()

    def edge_returns():
        edge_raw(1).wait_recv()
        edge_relay.wait_recv()
        edge_give[...] = for_end(edge_by, edge_first[...], edge_in[1], edge_in[2])
        edge_return(plane_slot).start()

    def edge_relays():
        edge_raw(0).wait_recv()
        edge_relay.start()

    @pl.when((chip == 1) & (odd == 0))
    def _():
        @pl.loop(0, AHEAD)
        def _(m):
            return_second(m)

        @pl.loop(0, split - AHEAD)
        def _(m):
            pass_on(m)
            return_second(m + AHEAD)

        @pl.loop(split - AHEAD, split)
        def _(m):
            pass_on(m)

        edge_returns()

        @pl.loop(split, messages)
        def _(m):
            pass_on(m)

        edge_relays()

    @pl.when((chip == 1) & (odd == 1))
    def _():
        @pl.loop(0, LAG)
        def _(m):
            pass_on(m)

        @pl.loop(0, messages - LAG)
        def _(m):
            return_second(m)
            pass_on(m + LAG)

        @pl.loop(messages - LAG, split)
        def _(m):
            return_second(m)

        edge_relays()
        edge_returns()

    @pl.when(chip == 1)
    def _():
        @pl.loop(0, split)
        def _(m):
            settle_second(m, False)

    def patch_fields():
        @pl.loop(0, rows // LANES)
        def _(block):
            where = pl.ds(pl.multiple_of(block * LANES, LANES), LANES)
            turned = edge_turn[:, where].T
            for plane in range(3):
                on_left = pltpu.roll(turned, (-16 * plane - 2) % LANES, 1)
                cut = pl.ds(0, LANES)
                out_fields[plane, where, cut] = jnp.where(
                    lane < 2, on_left, out_fields[plane, where, cut]
                )
                on_right = pltpu.roll(turned, (LANES - 2 - 16 * plane - 10) % LANES, 1)
                cut = pl.ds(cols - LANES, LANES)
                out_fields[plane, where, cut] = jnp.where(
                    lane >= LANES - 2, on_right, out_fields[plane, where, cut]
                )

    @pl.when(is_end)
    def _():
        patch_fields()

    def settle(m, late):
        where = span(m)
        by = of_row(moves, m, (MESSAGE, cols))
        slot = m - split + 2 if late else 0

        @pl.when(is_third)
        def _():
            raw(m, 1).wait_recv()
            relay(m).wait_recv()
            own = first[where, :]
            near = inbox[1, where, :]
            far = inbox[2, where, :]
            turn[where, :] = for_end(by, own, near, far)
            give(m, turn, 0).start()
            mine[where, :] = for_middle(by, own, inbox[0, where, :], near, far)
            swap(m, slot).start()

        @pl.when(is_leaf)
        def _():
            mine[where, :] = first[where, :]
            swap(m, slot).start()

        @pl.when(is_keeper)
        def _():
            flipped = of_row(flips, m, (MESSAGE, cols)) == 1
            parts = []
            for core in range(2):
                give(m, turn, core).wait_recv()
                part = back[core, where, :]
                if late:
                    far_direct(m, core).wait_recv()
                    part = jnp.where(by >= 2, inbox[1 + core, where, :], part)
                parts.append(part)
            settled = jnp.where(by == 0, first[where, :], parts[1])
            near_out[where, :] = jnp.where(flipped, settled, parts[0])
            pass_back(m, slot).start()
            mine[where, :] = jnp.where(flipped, parts[0], settled)

        @pl.when(chip == 3)
        def _():
            give(m, turn, 0).wait_recv()
            mine[where, :] = jnp.where(by == 0, first[where, :], back[0, where, :])
            swap(m, slot).start()

    @pl.when(chip != 1)
    def _():
        @pl.loop(0, split)
        def _(m):
            settle(m, False)

    def settle_edges():
        @pl.when(is_third)
        def _():
            edge_returns()

        @pl.when(is_middle)
        def _():
            edge_mine[...] = for_middle(
                edge_by, edge_first[...], edge_in[0], edge_in[1], edge_in[2]
            )
            edge_swap.start()

        @pl.when(is_leaf)
        def _():
            edge_mine[...] = edge_first[...]
            edge_swap.start()

        @pl.when(is_keeper)
        def _():
            for core in range(2):
                edge_return(core).wait_recv()
            flipped = by_line(flips) == 1
            settled = jnp.where(edge_by == 0, edge_first[...], edge_back[1])
            edge_near[...] = jnp.where(flipped, settled, edge_back[0])
            edge_pass.start()
            edge_mine[...] = jnp.where(flipped, edge_back[0], settled)

        @pl.when(chip == 3)
        def _():
            edge_return(0).wait_recv()
            edge_mine[...] = jnp.where(edge_by == 0, edge_first[...], edge_back[0])
            edge_swap.start()

    @pl.when(chip < 2)
    def _():
        settle_edges()

    @pl.when(chip != 1)
    def _():
        @pl.loop(split, messages)
        def _(m):
            settle(m, True)

    @pl.when(chip == 1)
    def _():
        @pl.loop(split, messages)
        def _(m):
            settle_second(m, True)

    @pl.when(chip >= 2)
    def _():
        settle_edges()

    @pl.when(is_middle)
    def _():
        patch_fields()

    edge_swap.wait_recv()
    choices = []
    for tile_row in range(tile_rows):
        still = jnp.where(moves[tile_row] == 0, 1, 0)
        flipped = flips[tile_row]
        from_leaf = flipped * still
        choice = jnp.where(is_keeper, from_leaf, flipped)
        choices.append(jnp.where(is_leaf, 1 - (1 - flipped) * still, choice))
    edge_final[0:8, :] = jnp.where(by_line(choices) == 1, edge_other[...], edge_mine[...])
    for tile_row in range(tile_rows):
        for block in range(tile // LANES):
            turned = edge_final[:, block * LANES : (block + 1) * LANES].T
            where = pl.ds(tile_row * tile + block * LANES, LANES)
            edge_wide[where, 0:LANES] = pltpu.roll(turned, (-4 * tile_row) % LANES, 1)
            edge_wide[where, cols - LANES : cols] = pltpu.roll(
                turned, (LANES - 2 - 4 * tile_row - 2) % LANES, 1
            )

    column = lax.broadcasted_iota(jnp.int32, (MESSAGE, cols), 1)
    inside = (column >= 2) & (column < cols - 2)

    early_rows = pl.ds(0, split * MESSAGE)
    remote(
        mine.at[early_rows, :], other.at[early_rows, :], swap_send.at[0], swap_recv.at[0], sibling
    ).wait_recv()

    @pl.loop(0, messages)
    def _(m):
        @pl.when(m >= split)
        def _():
            swap(m, m - split + 2).wait_recv()

        where = span(m)
        taken = of_row(choices, m, (MESSAGE, cols)) == 1
        value = jnp.where(taken, other[where, :], mine[where, :])
        out_depth[where, :] = jnp.where(inside, value, edge_wide[where, :])

    @pl.when((lead_left == 1) | (follow_left == 1))
    def _():
        halo_to_left.wait_send()

    @pl.when((lead_right == 1) | (follow_right == 1))
    def _():
        halo_to_right.wait_send()

    edge_raw(middle).wait_send()
    edge_swap.wait_send()

    remote(first, inbox.at[0], raw_send.at[0], in_recv.at[0, 0], toward).wait_send()
    remote(mine, other, swap_send.at[0], swap_recv.at[0], sibling).wait_send()

    @pl.when(is_middle)
    def _():
        edge_relay.wait_send()
        edge_return(plane_slot).wait_send()
        remote(inbox.at[0], inbox.at[2], relay_send.at[0], in_recv.at[2, 0], toward).wait_send()
        remote(turn, back.at[0], back_send.at[0], in_recv.at[0, 0], outward).wait_send()


def solution(mesh):
    axis = "gx"
    count = mesh.shape[axis]

    def body(fields, friction, wet_mask, owner_table):
        rows, cols = friction.shape
        padded = rows + 2 * PAD
        slots = rows // MESSAGE + 1
        f32 = jnp.float32
        whole = pltpu.VMEM((rows, cols), f32)
        small = pltpu.VMEM((8, cols), f32)
        scratch = [
            pltpu.VMEM((3, padded, cols), f32),
            pltpu.VMEM((padded, cols), f32),
            pltpu.VMEM((padded, cols), jnp.int32),
            pltpu.SMEM(owner_table.shape, jnp.int32),
            whole,
            pltpu.VMEM((3, rows, cols), f32),
            pltpu.VMEM((2, rows, cols), f32),
            whole,
            whole,
            whole,
            whole,
            whole,
            pltpu.VMEM((32, rows), f32),
            pltpu.VMEM((16, rows), f32),
            pltpu.VMEM((16, rows), f32),
            pltpu.VMEM((4, 16, rows), f32),
            pltpu.VMEM((LANES, rows), f32),
            small,
            pltpu.VMEM((3, 8, cols), f32),
            pltpu.VMEM((2, 8, cols), f32),
            small,
            small,
            small,
            small,
            pltpu.VMEM((LANES, cols), f32),
            whole,
            pltpu.SemaphoreType.DMA((2, 3)),
            pltpu.SemaphoreType.DMA,
            pltpu.SemaphoreType.DMA((2,)),
            pltpu.SemaphoreType.DMA((2,)),
            pltpu.SemaphoreType.DMA((3, slots)),
            pltpu.SemaphoreType.DMA((2,)),
            pltpu.SemaphoreType.DMA((2,)),
            pltpu.SemaphoreType.DMA((2 + DIRECT,)),
            pltpu.SemaphoreType.DMA((2,)),
            pltpu.SemaphoreType.DMA((2,)),
            pltpu.SemaphoreType.REGULAR,
        ]
        arrays = [
            pltpu.with_memory_space_constraint(array, pltpu.HBM)
            for array in (fields, friction, wet_mask, owner_table)
        ]
        return pl.pallas_call(
            functools.partial(kernel, axis, count),
            out_shape=(
                jax.ShapeDtypeStruct(fields.shape, f32),
                jax.ShapeDtypeStruct(friction.shape, f32),
            ),
            in_specs=[pl.BlockSpec(memory_space=pltpu.HBM)] * 4,
            out_specs=(
                pl.BlockSpec(memory_space=pltpu.VMEM),
                pl.BlockSpec(memory_space=pltpu.VMEM),
            ),
            scratch_shapes=scratch,
            compiler_params=pltpu.CompilerParams(
                collective_id=0, has_side_effects=True, vmem_limit_bytes=32 * 2**20
            ),
            name="shallow_water",
        )(*arrays)

    in_specs = (P(None, "groups", axis), P("groups", axis), P("groups", axis), P("groups", None))
    out_specs = (P(None, "groups", axis), P("groups", axis))
    return jax.shard_map(body, mesh=mesh, in_specs=in_specs, out_specs=out_specs, check_vma=False)
```

time: 42.8 us -> 36.5 us (0.85)
  Pallas kernels: 40.1 us -> 33.8 us
    pallas_call x1, Pallas kernels: 40.1 us -> 33.8 us  [body(): pl.pallas_call(functools.partial(kernel, axis, count), out_shape=(jax.Sha...]
where the time goes in v4:
time: 36.5 us; the launch traced here: 36.4 us
  Pallas kernels  33.8 us (93%)
  local copies, waits for them, and re-layouts  1.94 us (5%)
  between operations  0.64 us (2%)
    pallas_call x1, Pallas kernels, body(): pl.pallas_call(functools.partial(kernel, axis, count), out_shape=(jax.Sha...  33.8 us
    unnamed x2, local copies, waits for them, and re-layouts  1.94 us

profile of v4, /device:TPU:513, one launch (start us, length us, event | category | flops | bytes accessed | tf_op | source)
XLA Modules:
  0.0 36.4 jit_solution(7187538288848203643)
XLA Ops:
  0.6 33.8 %shallow_water.1 = (f32[3,512,256]{2,1,0:T(8,128)S(1)}, f32[512,256]{1,0:T(8,128)S(1)}) custom-call(f32[3,512,256]{2,1,0:T(8,128)} %fields_ref.1, f32[512,256]{1,0:T(8,128)} %friction_ref.1, s32[512,256]{1,0:T(8,128)} %wet_ref.1, s32[2,128]{1,0:T(2,128)} %owner_ref.1), custom_call_target="tpu_custom_call" | custom-call | tf_op jit(solution)/shard_map/shallow_water/pallas_call | solution.py:786
  34.4 1.1 %copy.8 = f32[3,512,256]{2,1,0:T(8,128)} copy(f32[3,512,256]{2,1,0:T(8,128)S(1)} %get-tuple-element.4) | data formatting | bytes 3145728
  35.6 0.8 %copy.9 = f32[512,256]{1,0:T(8,128)} copy(f32[512,256]{1,0:T(8,128)S(1)} %get-tuple-element.5) | data formatting | bytes 1048576

commit v5 on v4

--- a/solution.py
+++ b/solution.py
@@ -12,9 +12,9 @@
 CHUNK = 64
 MESSAGE = 32
 LAG = 8
-AHEAD = 6
+AHEAD = 8
 DIRECT = 4
-FIRST = 128
+FIRST = 80
 LANES = 128
 
 gravity_half = 0.5
@@ -84,6 +84,7 @@
     edge_back,
     edge_give,
     edge_near,
+    edge_far,
     edge_mine,
     edge_other,
     edge_final,
@@ -256,9 +257,20 @@
         edge_in.at[0], edge_in.at[2], relay_send.at[1], in_recv.at[2, extra], toward
     )
 
-    def edge_return(slot):
+    def edge_return(slot, source):
+        return remote(source, edge_back.at[slot], back_send.at[1], in_recv.at[slot, extra], receiver)
+
+    edge_near_direct = remote(
+        edge_near, edge_in.at[1], raw_send.at[1], in_recv.at[1, extra], me - 2
+    )
+
+    def edge_far_direct(core):
         return remote(
-            edge_give, edge_back.at[slot], back_send.at[1], in_recv.at[slot, extra], receiver
+            edge_far,
+            edge_in.at[1 + core],
+            relay_send.at[1],
+            in_recv.at[2, extra - (1 - core) * split],
+            keeper,
         )
 
     edge_pass = remote(edge_near, edge_other, swap_send.at[1], swap_recv.at[1], sibling)
@@ -438,7 +450,14 @@
         cut = pl.ds(tile_row * tile, tile)
         edge_first[4 * tile_row : 4 * tile_row + 2, :] = edge_turn[2:4, cut]
         edge_first[4 * tile_row + 2 : 4 * tile_row + 4, :] = edge_turn[10:12, cut]
-    edge_raw(middle).start()
+
+    @pl.when(chip != 2)
+    def _():
+        edge_raw(middle).start()
+
+    @pl.when(chip == 1)
+    def _():
+        edge_return(plane_slot, edge_first).start()
 
     line = lax.broadcasted_iota(jnp.int32, (8, cols), 0)
 
@@ -475,8 +494,11 @@
     @pl.when(is_third)
     def _():
         edge_raw(0).wait_recv()
-        edge_relay.start()
+        edge_near[...] = jnp.where(edge_by == 3, edge_first[...], edge_in[0])
+        edge_near_direct.start()
         pl.semaphore_wait(hello, 1)
+        edge_far[...] = jnp.where(edge_by == 2, edge_first[...], edge_in[0])
+        edge_far_direct(odd).start()
 
         @pl.loop(split, messages)
         def _(m):
@@ -485,12 +507,6 @@
             far_out[where, :] = jnp.where(by == 2, first[where, :], inbox[0, where, :])
             far_direct(m, odd).start()
 
-    def edge_returns():
-        edge_raw(1).wait_recv()
-        edge_relay.wait_recv()
-        edge_give[...] = for_end(edge_by, edge_first[...], edge_in[1], edge_in[2])
-        edge_return(plane_slot).start()
-
     def edge_relays():
         edge_raw(0).wait_recv()
         edge_relay.start()
@@ -506,13 +522,7 @@
             pass_on(m)
             return_second(m + AHEAD)
 
-        @pl.loop(split - AHEAD, split)
-        def _(m):
-            pass_on(m)
-
-        edge_returns()
-
-        @pl.loop(split, messages)
+        @pl.loop(split - AHEAD, messages)
         def _(m):
             pass_on(m)
 
@@ -534,7 +544,6 @@
             return_second(m)
 
         edge_relays()
-        edge_returns()
 
     @pl.when(chip == 1)
     def _():
@@ -616,13 +625,21 @@
     def settle_edges():
         @pl.when(is_third)
         def _():
-            edge_returns()
-
-        @pl.when(is_middle)
-        def _():
-            edge_mine[...] = for_middle(
-                edge_by, edge_first[...], edge_in[0], edge_in[1], edge_in[2]
-            )
+            edge_raw(1).wait_recv()
+            edge_relay.wait_recv()
+            own = edge_first[...]
+            near = edge_in[1]
+            far = edge_in[2]
+            edge_give[...] = for_end(edge_by, own, near, far)
+            edge_return(0, edge_give).start()
+            edge_mine[...] = for_middle(edge_by, own, edge_in[0], near, far)
+            edge_swap.start()
+
+        @pl.when(chip == 1)
+        def _():
+            edge_raw(1).wait_recv()
+            end_or_own = jnp.where(edge_by == 1, edge_in[0], edge_first[...])
+            edge_mine[...] = jnp.where(edge_by >= 2, edge_in[1], end_or_own)
             edge_swap.start()
 
         @pl.when(is_leaf)
@@ -632,17 +649,20 @@
 
         @pl.when(is_keeper)
         def _():
+            parts = []
             for core in range(2):
-                edge_return(core).wait_recv()
+                edge_return(core, edge_give).wait_recv()
+                edge_far_direct(core).wait_recv()
+                parts.append(jnp.where(edge_by >= 2, edge_in[1 + core], edge_back[core]))
             flipped = by_line(flips) == 1
-            settled = jnp.where(edge_by == 0, edge_first[...], edge_back[1])
-            edge_near[...] = jnp.where(flipped, settled, edge_back[0])
+            settled = jnp.where(edge_by == 0, edge_first[...], parts[1])
+            edge_near[...] = jnp.where(flipped, settled, parts[0])
             edge_pass.start()
-            edge_mine[...] = jnp.where(flipped, edge_back[0], settled)
+            edge_mine[...] = jnp.where(flipped, parts[0], settled)
 
         @pl.when(chip == 3)
         def _():
-            edge_return(0).wait_recv()
+            edge_return(0, edge_give).wait_recv()
             edge_mine[...] = jnp.where(edge_by == 0, edge_first[...], edge_back[0])
             edge_swap.start()
 
@@ -724,9 +744,22 @@
     @pl.when(is_middle)
     def _():
         edge_relay.wait_send()
-        edge_return(plane_slot).wait_send()
+        edge_return(plane_slot, edge_give).wait_send()
         remote(inbox.at[0], inbox.at[2], relay_send.at[0], in_recv.at[2, 0], toward).wait_send()
         remote(turn, back.at[0], back_send.at[0], in_recv.at[0, 0], outward).wait_send()
+
+
+def flush(fields_ref, depth_ref, out_fields, out_depth, sem):
+    copies = [
+        pltpu.make_async_copy(depth_ref, out_depth, sem.at[3]),
+    ] + [
+        pltpu.make_async_copy(fields_ref.at[plane], out_fields.at[plane], sem.at[plane])
+        for plane in range(3)
+    ]
+    for copy in copies:
+        copy.start()
+    for copy in copies:
+        copy.wait()
 
 
 def solution(mesh):
@@ -765,6 +798,7 @@
             small,
             small,
             small,
+            small,
             pltpu.VMEM((LANES, cols), f32),
             whole,
             pltpu.SemaphoreType.DMA((2, 3)),
@@ -783,7 +817,7 @@
             pltpu.with_memory_space_constraint(array, pltpu.HBM)
             for array in (fields, friction, wet_mask, owner_table)
         ]
-        return pl.pallas_call(
+        results = pl.pallas_call(
             functools.partial(kernel, axis, count),
             out_shape=(
                 jax.ShapeDtypeStruct(fields.shape, f32),
@@ -800,6 +834,21 @@
             ),
             name="shallow_water",
         )(*arrays)
+        return pl.pallas_call(
+            flush,
+            out_shape=(
+                jax.ShapeDtypeStruct(fields.shape, f32),
+                jax.ShapeDtypeStruct(friction.shape, f32),
+            ),
+            in_specs=[pl.BlockSpec(memory_space=pltpu.VMEM)] * 2,
+            out_specs=(
+                pl.BlockSpec(memory_space=pltpu.HBM),
+                pl.BlockSpec(memory_space=pltpu.HBM),
+            ),
+            scratch_shapes=[pltpu.SemaphoreType.DMA((4,))],
+            compiler_params=pltpu.CompilerParams(vmem_limit_bytes=32 * 2**20),
+            name="flush",
+        )(*results)
 
     in_specs = (P(None, "groups", axis), P("groups", axis), P("groups", axis), P("groups", None))
     out_specs = (P(None, "groups", axis), P("groups", axis))

time: 36.5 us -> 35.2 us (0.964)
  local copies, waits for them, and re-layouts: 1.94 us -> 0 us
  Pallas kernels: 33.8 us -> 34.2 us
    unnamed x2 -> x0, local copies, waits for them, and re-layouts: 1.94 us -> none
    pallas_call x0 -> x1, Pallas kernels: none -> 1.35 us  [body(): pl.pallas_call(flush, out_shape=(jax.ShapeDtypeStruct(fields.shape, f32),...]
    pallas_call x1, Pallas kernels: 33.8 us -> 32.9 us  [body(): pl.pallas_call(functools.partial(kernel, axis, count), out_shape=(jax.Sha...]
where the time goes in v5:
time: 35.2 us; the launch traced here: 34.9 us
  Pallas kernels  34.2 us (97%)
  between operations  0.64 us (2%)
    pallas_call x1, Pallas kernels, body(): pl.pallas_call(functools.partial(kernel, axis, count), out_shape=(jax.Sha...  32.9 us
    pallas_call x1, Pallas kernels, body(): pl.pallas_call(flush, out_shape=(jax.ShapeDtypeStruct(fields.shape, f32),...  1.35 us

profile of v5, /device:TPU:513, one launch (start us, length us, event | category | flops | bytes accessed | tf_op | source)
XLA Modules:
  0.0 34.9 jit_solution(5433835427587293600)
XLA Ops:
  0.6 32.9 %shallow_water.1 = (f32[3,512,256]{2,1,0:T(8,128)S(1)}, f32[512,256]{1,0:T(8,128)S(1)}) custom-call(f32[3,512,256]{2,1,0:T(8,128)} %fields_ref.1, f32[512,256]{1,0:T(8,128)} %friction_ref.1, s32[512,256]{1,0:T(8,128)} %wet_ref.1, s32[2,128]{1,0:T(2,128)} %owner_ref.1), custom_call_target="tpu_custom_call" | custom-call | tf_op jit(solution)/shard_map/shallow_water/pallas_call | solution.py:820
  33.5 1.3 %flush.1 = (f32[3,512,256]{2,1,0:T(8,128)}, f32[512,256]{1,0:T(8,128)}) custom-call(f32[3,512,256]{2,1,0:T(8,128)S(1)} %get-tuple-element.4.fields_ref, f32[512,256]{1,0:T(8,128)S(1)} %get-tuple-element.5.depth_ref), custom_call_target="tpu_custom_call" | custom-call | tf_op jit(solution)/shard_map/flush/pallas_call | solution.py:837

commit v6 on v5

--- a/solution.py
+++ b/solution.py
@@ -75,6 +75,7 @@
     mine,
     other,
     packed,
+    outer,
     halo_left,
     halo_right,
     edge,
@@ -150,10 +151,8 @@
             copy.wait()
 
     table = pltpu.make_async_copy(owner_ref, owner, table_sem)
-    for number in range(2):
-        for copy in load(number):
-            copy.start()
-    table.start()
+    for copy in load(0):
+        copy.start()
 
     barrier = pltpu.get_barrier_semaphore()
 
@@ -183,6 +182,9 @@
             state[plane, start : start + PAD, :] = zero_rows
         fric[start : start + PAD, :] = zero_rows
         mask[start : start + PAD, :] = jnp.zeros((PAD, cols), jnp.int32)
+    for copy in load(1):
+        copy.start()
+    table.start()
     edge[...] = jnp.zeros_like(edge)
     edge_turn[...] = jnp.zeros_like(edge_turn)
     edge_final[...] = jnp.zeros_like(edge_final)
@@ -277,18 +279,17 @@
     edge_swap = remote(edge_mine, edge_other, swap_send.at[1], swap_recv.at[1], sibling)
 
     halo_to_left = remote(
-        packed.at[pl.ds(0, 16), :], halo_right, halo_send.at[0], halo_recv.at[0], me - 1
+        outer.at[pl.ds(0, 8), :], halo_right, halo_send.at[0], halo_recv.at[0], me - 1
     )
     halo_to_right = remote(
-        packed.at[pl.ds(16, 16), :], halo_left, halo_send.at[1], halo_recv.at[1], me + 1
+        outer.at[pl.ds(8, 8), :], halo_left, halo_send.at[1], halo_recv.at[1], me + 1
     )
 
     def shift(axis_number, amount, size):
         return lambda a: pltpu.roll(a, amount % size, axis_number)
 
-    def compute(i):
-        reach = CHUNK + 2 * PAD
-        at = pl.multiple_of(i * CHUNK, CHUNK)
+    def compute(at, size):
+        reach = size + 2 * PAD
         where = pl.ds(at, reach)
         openness = mask[where, :].astype(jnp.float32) * fric[where, :]
         wet, damping = masks(openness)
@@ -303,10 +304,10 @@
                 shift(0, -1, reach),
                 shift(0, 1, reach),
             )
-        here = pl.ds(at, CHUNK)
-        first[here, :] = values[0][PAD : PAD + CHUNK]
+        here = pl.ds(at, size)
+        first[here, :] = values[0][PAD : PAD + size]
         for plane in range(3):
-            out_fields[plane, here, :] = values[plane][PAD : PAD + CHUNK]
+            out_fields[plane, here, :] = values[plane][PAD : PAD + size]
 
     def for_end(by, own, near, far):
         return jnp.where(by == 3, far, jnp.where(by == 2, near, own))
@@ -331,19 +332,22 @@
             pl.semaphore_signal(hello, inc=1, device_id={axis: me + ahead}, device_id_type=MESH)
 
     await_load(0)
-    compute(0)
+    compute(0, MESSAGE)
 
     @pl.when(position != 1)
     def _():
         pl.semaphore_wait(barrier, 1 + lead_left + lead_right)
 
-    send_chunk(0)
+    raw(0, middle).start()
+    for part in range(1, CHUNK // MESSAGE):
+        compute(part * MESSAGE, MESSAGE)
+        raw(part, middle).start()
     await_load(1)
     table.wait()
     moves = [differs(tile_row, 1) + 2 * differs(tile_row, 2) for tile_row in range(tile_rows)]
     flips = [differs(tile_row, 0) for tile_row in range(tile_rows)]
 
-    compute(1)
+    compute(CHUNK, CHUNK)
     send_chunk(1)
 
     lane = lax.broadcasted_iota(jnp.int32, (LANES, LANES), 1)
@@ -362,7 +366,12 @@
                 target = 16 * side + 4 * number
                 moved = pltpu.roll(values, (target - source) % LANES, 1)
                 result = jnp.where(lane >= target, moved, result)
-        packed[:, pl.ds(pl.multiple_of(block * LANES, LANES), LANES)] = result.T[0:32]
+        turned = result.T[0:32]
+        there = pl.ds(pl.multiple_of(block * LANES, LANES), LANES)
+        packed[:, there] = turned
+        for number in range(4):
+            outer[2 * number : 2 * number + 2, there] = turned[4 * number : 4 * number + 2]
+            outer[8 + 2 * number : 10 + 2 * number, there] = turned[18 + 4 * number : 20 + 4 * number]
 
     @pl.when(lead_left == 1)
     def _():
@@ -374,7 +383,7 @@
 
     @pl.loop(2, chunks)
     def _(j):
-        compute(j)
+        compute(pl.multiple_of(j * CHUNK, CHUNK), CHUNK)
 
         @pl.when((chip != 2) | (j < split * MESSAGE // CHUNK))
         def _():
@@ -426,10 +435,11 @@
 
     for number in range(4):
         base = 4 * number
-        edge[number, 0:2, :] = jnp.where(me > 0, halo_left[base + 2 : base + 4, :], 0.0)
+        pair = pl.ds(2 * number, 2)
+        edge[number, 0:2, :] = jnp.where(me > 0, halo_left[pair, :], 0.0)
         edge[number, 2:6, :] = packed[base : base + 4, :]
         edge[number, 8:12, :] = packed[16 + base : 20 + base, :]
-        edge[number, 12:14, :] = jnp.where(me < count - 1, halo_right[base : base + 2, :], 0.0)
+        edge[number, 12:14, :] = jnp.where(me < count - 1, halo_right[pair, :], 0.0)
 
     place = lax.broadcasted_iota(jnp.int32, (16, rows), 1)
     wet, damping = masks(edge[3])
@@ -522,11 +532,13 @@
             pass_on(m)
             return_second(m + AHEAD)
 
-        @pl.loop(split - AHEAD, messages)
+        @pl.loop(split - AHEAD, messages - 2)
         def _(m):
             pass_on(m)
 
         edge_relays()
+        for m in range(messages - 2, messages):
+            pass_on(m)
 
     @pl.when((chip == 1) & (odd == 1))
     def _():
@@ -666,66 +678,89 @@
             edge_mine[...] = jnp.where(edge_by == 0, edge_first[...], edge_back[0])
             edge_swap.start()
 
-    @pl.when(chip < 2)
-    def _():
-        settle_edges()
-
-    @pl.when(chip != 1)
-    def _():
-        @pl.loop(split, messages)
-        def _(m):
-            settle(m, True)
-
-    @pl.when(chip == 1)
-    def _():
-        @pl.loop(split, messages)
-        def _(m):
-            settle_second(m, True)
-
-    @pl.when(chip >= 2)
-    def _():
-        settle_edges()
-
-    @pl.when(is_middle)
-    def _():
-        patch_fields()
-
-    edge_swap.wait_recv()
     choices = []
     for tile_row in range(tile_rows):
         still = jnp.where(moves[tile_row] == 0, 1, 0)
         flipped = flips[tile_row]
-        from_leaf = flipped * still
-        choice = jnp.where(is_keeper, from_leaf, flipped)
+        choice = jnp.where(is_keeper, flipped * still, flipped)
         choices.append(jnp.where(is_leaf, 1 - (1 - flipped) * still, choice))
-    edge_final[0:8, :] = jnp.where(by_line(choices) == 1, edge_other[...], edge_mine[...])
-    for tile_row in range(tile_rows):
-        for block in range(tile // LANES):
-            turned = edge_final[:, block * LANES : (block + 1) * LANES].T
-            where = pl.ds(tile_row * tile + block * LANES, LANES)
-            edge_wide[where, 0:LANES] = pltpu.roll(turned, (-4 * tile_row) % LANES, 1)
-            edge_wide[where, cols - LANES : cols] = pltpu.roll(
-                turned, (LANES - 2 - 4 * tile_row - 2) % LANES, 1
-            )
 
     column = lax.broadcasted_iota(jnp.int32, (MESSAGE, cols), 1)
     inside = (column >= 2) & (column < cols - 2)
 
-    early_rows = pl.ds(0, split * MESSAGE)
-    remote(
-        mine.at[early_rows, :], other.at[early_rows, :], swap_send.at[0], swap_recv.at[0], sibling
-    ).wait_recv()
-
-    @pl.loop(0, messages)
-    def _(m):
-        @pl.when(m >= split)
-        def _():
-            swap(m, m - split + 2).wait_recv()
-
+    def deliver(m):
         where = span(m)
         taken = of_row(choices, m, (MESSAGE, cols)) == 1
         value = jnp.where(taken, other[where, :], mine[where, :])
         out_depth[where, :] = jnp.where(inside, value, edge_wide[where, :])
+
+    def deliver_early():
+        edge_swap.wait_recv()
+        edge_final[0:8, :] = jnp.where(by_line(choices) == 1, edge_other[...], edge_mine[...])
+        for tile_row in range(tile_rows):
+            for block in range(tile // LANES):
+                turned = edge_final[:, block * LANES : (block + 1) * LANES].T
+                where = pl.ds(tile_row * tile + block * LANES, LANES)
+                edge_wide[where, 0:LANES] = pltpu.roll(turned, (-4 * tile_row) % LANES, 1)
+                edge_wide[where, cols - LANES : cols] = pltpu.roll(
+                    turned, (LANES - 2 - 4 * tile_row - 2) % LANES, 1
+                )
+        early_rows = pl.ds(0, split * MESSAGE)
+        remote(
+            mine.at[early_rows, :], other.at[early_rows, :], swap_send.at[0], swap_recv.at[0], sibling
+        ).wait_recv()
+
+        @pl.loop(0, split)
+        def _(m):
+            deliver(m)
+
+    @pl.when(chip == 0)
+    def _():
+        settle_edges()
+        deliver_early()
+
+        @pl.loop(split, messages)
+        def _(m):
+            settle(m, True)
+
+    @pl.when(chip == 1)
+    def _():
+        settle_edges()
+
+        @pl.loop(split, messages)
+        def _(m):
+            settle_second(m, True)
+
+        patch_fields()
+        deliver_early()
+
+    @pl.when(is_third)
+    def _():
+        @pl.loop(split, messages - 2)
+        def _(m):
+            settle(m, True)
+
+        settle_edges()
+        for m in range(messages - 2, messages):
+            settle(m, True)
+        patch_fields()
+        deliver_early()
+
+    @pl.when(chip == 3)
+    def _():
+        @pl.loop(split, messages - 2)
+        def _(m):
+            settle(m, True)
+
+        settle_edges()
+        for m in range(messages - 2, messages):
+            settle(m, True)
+        deliver_early()
+
+    @pl.loop(split, messages)
+    def _(m):
+        swap(m, m - split + 2).wait_recv()
+        deliver(m)
 
     @pl.when((lead_left == 1) | (follow_left == 1))
     def _():
@@ -788,7 +823,8 @@
             whole,
             pltpu.VMEM((32, rows), f32),
             pltpu.VMEM((16, rows), f32),
-            pltpu.VMEM((16, rows), f32),
+            pltpu.VMEM((8, rows), f32),
+            pltpu.VMEM((8, rows), f32),
             pltpu.VMEM((4, 16, rows), f32),
             pltpu.VMEM((LANES, rows), f32),
             small,

time: 35.2 us -> 34.8 us (0.989)
  no operation moved by 1% of the time
where the time goes in v6:
time: 34.8 us; the launch traced here: 34.6 us
  Pallas kernels  34 us (98%)
  between operations  0.64 us (2%)
    pallas_call x1, Pallas kernels, body(): pl.pallas_call(functools.partial(kernel, axis, count), out_shape=(jax.Sha...  32.7 us
    pallas_call x1, Pallas kernels, body(): pl.pallas_call(flush, out_shape=(jax.ShapeDtypeStruct(fields.shape, f32),...  1.35 us

profile of v6, /device:TPU:513, one launch (start us, length us, event | category | flops | bytes accessed | tf_op | source)
XLA Modules:
  0.0 34.6 jit_solution(10758490110939602419)
XLA Ops:
  0.6 32.7 %shallow_water.1 = (f32[3,512,256]{2,1,0:T(8,128)S(1)}, f32[512,256]{1,0:T(8,128)S(1)}) custom-call(f32[3,512,256]{2,1,0:T(8,128)} %fields_ref.1, f32[512,256]{1,0:T(8,128)} %friction_ref.1, s32[512,256]{1,0:T(8,128)} %wet_ref.1, s32[2,128]{1,0:T(2,128)} %owner_ref.1), custom_call_target="tpu_custom_call" | custom-call | tf_op jit(solution)/shard_map/shallow_water/pallas_call | solution.py:856
  33.3 1.3 %flush.1 = (f32[3,512,256]{2,1,0:T(8,128)}, f32[512,256]{1,0:T(8,128)}) custom-call(f32[3,512,256]{2,1,0:T(8,128)S(1)} %get-tuple-element.4.fields_ref, f32[512,256]{1,0:T(8,128)S(1)} %get-tuple-element.5.depth_ref), custom_call_target="tpu_custom_call" | custom-call | tf_op jit(solution)/shard_map/flush/pallas_call | solution.py:873

commit v7 on v6

--- a/solution.py
+++ b/solution.py
@@ -499,7 +499,7 @@
             mine[where, :] = jnp.where(by >= 2, near, jnp.where(by == 1, end, own))
         else:
             mine[where, :] = for_middle(by, own, end, near, inbox[2, where, :])
-        swap(m, m - split + 2 if late else 0).start()
+        swap(m, 2 if late else 0).start()
 
     @pl.when(is_third)
     def _():
@@ -587,7 +587,7 @@
     def settle(m, late):
         where = span(m)
         by = of_row(moves, m, (MESSAGE, cols))
-        slot = m - split + 2 if late else 0
+        slot = 2 if late else 0
 
         @pl.when(is_third)
         def _():
@@ -685,12 +685,11 @@
         choice = jnp.where(is_keeper, flipped * still, flipped)
         choices.append(jnp.where(is_leaf, 1 - (1 - flipped) * still, choice))
 
-    column = lax.broadcasted_iota(jnp.int32, (MESSAGE, cols), 1)
-    inside = (column >= 2) & (column < cols - 2)
-
-    def deliver(m):
-        where = span(m)
-        taken = of_row(choices, m, (MESSAGE, cols)) == 1
+    def deliver(m, size=MESSAGE):
+        where = pl.ds(pl.multiple_of(m * MESSAGE, MESSAGE), size)
+        column = lax.broadcasted_iota(jnp.int32, (size, cols), 1)
+        inside = (column >= 2) & (column < cols - 2)
+        taken = of_row(choices, m, (size, cols)) == 1
         value = jnp.where(taken, other[where, :], mine[where, :])
         out_depth[where, :] = jnp.where(inside, value, edge_wide[where, :])
 
@@ -757,10 +756,12 @@
             settle(m, True)
         deliver_early()
 
-    @pl.loop(split, messages)
-    def _(m):
-        swap(m, m - split + 2).wait_recv()
-        deliver(m)
+    start = split * MESSAGE
+    late_rows = pl.ds(start, rows - start)
+    remote(
+        mine.at[late_rows, :], other.at[late_rows, :], swap_send.at[0], swap_recv.at[2], sibling
+    ).wait_recv()
+    deliver(split, rows - start)
 
     @pl.when((lead_left == 1) | (follow_left == 1))
     def _():
@@ -786,10 +787,8 @@
 
 def flush(fields_ref, depth_ref, out_fields, out_depth, sem):
     copies = [
-        pltpu.make_async_copy(depth_ref, out_depth, sem.at[3]),
-    ] + [
-        pltpu.make_async_copy(fields_ref.at[plane], out_fields.at[plane], sem.at[plane])
-        for plane in range(3)
+        pltpu.make_async_copy(depth_ref, out_depth, sem.at[0]),
+        pltpu.make_async_copy(fields_ref, out_fields, sem.at[1]),
     ]
     for copy in copies:
         copy.start()
@@ -844,7 +843,7 @@
             pltpu.SemaphoreType.DMA((3, slots)),
             pltpu.SemaphoreType.DMA((2,)),
             pltpu.SemaphoreType.DMA((2,)),
-            pltpu.SemaphoreType.DMA((2 + DIRECT,)),
+            pltpu.SemaphoreType.DMA((3,)),
             pltpu.SemaphoreType.DMA((2,)),
             pltpu.SemaphoreType.DMA((2,)),
             pltpu.SemaphoreType.REGULAR,
@@ -881,7 +880,7 @@
                 pl.BlockSpec(memory_space=pltpu.HBM),
                 pl.BlockSpec(memory_space=pltpu.HBM),
             ),
-            scratch_shapes=[pltpu.SemaphoreType.DMA((4,))],
+            scratch_shapes=[pltpu.SemaphoreType.DMA((2,))],
             compiler_params=pltpu.CompilerParams(vmem_limit_bytes=32 * 2**20),
             name="flush",
         )(*results)

time: 34.8 us -> 34.7 us (level)
  no operation moved by 1% of the time
where the time goes in v7:
time: 34.7 us; the launch traced here: 34.6 us
  Pallas kernels  34 us (98%)
  between operations  0.64 us (2%)
    pallas_call x1, Pallas kernels, body(): pl.pallas_call(functools.partial(kernel, axis, count), out_shape=(jax.Sha...  32.6 us
    pallas_call x1, Pallas kernels, body(): pl.pallas_call(flush, out_shape=(jax.ShapeDtypeStruct(fields.shape, f32),...  1.33 us

profile of v7, /device:TPU:513, one launch (start us, length us, event | category | flops | bytes accessed | tf_op | source)
XLA Modules:
  0.0 34.6 jit_solution(8976233231532131717)
XLA Ops:
  0.6 32.6 %shallow_water.1 = (f32[3,512,256]{2,1,0:T(8,128)S(1)}, f32[512,256]{1,0:T(8,128)S(1)}) custom-call(f32[3,512,256]{2,1,0:T(8,128)} %fields_ref.1, f32[512,256]{1,0:T(8,128)} %friction_ref.1, s32[512,256]{1,0:T(8,128)} %wet_ref.1, s32[2,128]{1,0:T(2,128)} %owner_ref.1), custom_call_target="tpu_custom_call" | custom-call | tf_op jit(solution)/shard_map/shallow_water/pallas_call | solution.py:855
  33.3 1.3 %flush.1 = (f32[3,512,256]{2,1,0:T(8,128)}, f32[512,256]{1,0:T(8,128)}) custom-call(f32[3,512,256]{2,1,0:T(8,128)S(1)} %get-tuple-element.4.fields_ref, f32[512,256]{1,0:T(8,128)S(1)} %get-tuple-element.5.depth_ref), custom_call_target="tpu_custom_call" | custom-call | tf_op jit(solution)/shard_map/flush/pallas_call | solution.py:872

commit v8 on v7

--- a/solution.py
+++ b/solution.py
@@ -12,8 +12,8 @@
 CHUNK = 64
 MESSAGE = 32
 LAG = 8
-AHEAD = 8
-DIRECT = 4
+AHEAD = 10
+DIRECT = 6
 FIRST = 80
 LANES = 128
 

time: 34.7 us -> 34.7 us (level)
  no operation moved by 1% of the time
where the time goes in v8:
time: 34.7 us; the launch traced here: 34.5 us
  Pallas kernels  33.9 us (98%)
  between operations  0.64 us (2%)
    pallas_call x1, Pallas kernels, body(): pl.pallas_call(functools.partial(kernel, axis, count), out_shape=(jax.Sha...  32.6 us
    pallas_call x1, Pallas kernels, body(): pl.pallas_call(flush, out_shape=(jax.ShapeDtypeStruct(fields.shape, f32),...  1.33 us

profile of v8, /device:TPU:513, one launch (start us, length us, event | category | flops | bytes accessed | tf_op | source)
XLA Modules:
  0.0 34.5 jit_solution(3246658763643809246)
XLA Ops:
  0.6 32.6 %shallow_water.1 = (f32[3,512,256]{2,1,0:T(8,128)S(1)}, f32[512,256]{1,0:T(8,128)S(1)}) custom-call(f32[3,512,256]{2,1,0:T(8,128)} %fields_ref.1, f32[512,256]{1,0:T(8,128)} %friction_ref.1, s32[512,256]{1,0:T(8,128)} %wet_ref.1, s32[2,128]{1,0:T(2,128)} %owner_ref.1), custom_call_target="tpu_custom_call" | custom-call | tf_op jit(solution)/shard_map/shallow_water/pallas_call | solution.py:855
  33.2 1.3 %flush.1 = (f32[3,512,256]{2,1,0:T(8,128)}, f32[512,256]{1,0:T(8,128)}) custom-call(f32[3,512,256]{2,1,0:T(8,128)S(1)} %get-tuple-element.4.fields_ref, f32[512,256]{1,0:T(8,128)S(1)} %get-tuple-element.5.depth_ref), custom_call_target="tpu_custom_call" | custom-call | tf_op jit(solution)/shard_map/flush/pallas_call | solution.py:872
